TPU v7x, 32 devices: a whole 2x2x4 slice. The times are simulated.
32 devices in a mesh: member: 2 (over y), gx: 4 (over z), gy: 4 (over x, core).
Axes of the slice: x: 2, y: 2, z: 4, core: 2. Of those that a mesh axis runs over, the one named last changes fastest.
Arguments:
- populations: float32 [19, 32, 64, 128], P(None, ('member', 'gx'), 'gy'), parts along dimension 1, may hold values from 0 to 1, as said below
- heat_level: int32 [32, 64, 128], P(('member', 'gx'), 'gy'), parts along dimension 0, may hold values from 0 to 7
- obstacle: int32 [32, 64, 128], P(('member', 'gx'), 'gy'), parts along dimension 0, may hold values 0 or 1
- heat_table: float32 [8], replicated, may hold values from 0.02 to 0.5
Outputs:
- final_populations: float32 [19, 32, 64, 128], P(None, ('member', 'gx'), 'gy'), parts along dimension 1
- velocity: float32 [3, 32, 64, 128], P(None, ('member', 'gx'), 'gy'), parts along dimension 1
There are 2 independent parts, one for each index of `member`. A program takes and returns all parts, laid end to end along the dimension named above; an argument that names none is the same for every part. Nothing has to cross between parts.
Inputs may be any that keep to these rules, and one draw needn't show every extreme that they name: Positive populations near a local equilibrium, in the direction order of the steps.
All inputs are finite; a program needn't handle non-finite values. No bound on the sum of `obstacle` on one device may be relied on, other than what follows from the above.
Results may differ from a plain program's by a relative error of at most 0.0001.
Values sent between devices are 32-bit elements; how exact they have to be, the bound alone decides.
A program may use at most 64 MiB of HBM per device.

v0:
```python
import functools

import jax
import jax.numpy as jnp
import numpy as np
from jax import lax
from jax.experimental import pallas as pl
from jax.experimental.pallas import tpu as pltpu
from jax.sharding import PartitionSpec as P

STEPS = 2
ROW = 8

lattice = np.array(
    [
        [0, 0, 0],
        [1, 0, 0],
        [-1, 0, 0],
        [0, 1, 0],
        [0, -1, 0],
        [0, 0, 1],
        [0, 0, -1],
        [1, 1, 0],
        [-1, -1, 0],
        [1, -1, 0],
        [-1, 1, 0],
        [1, 0, 1],
        [-1, 0, -1],
        [1, 0, -1],
        [-1, 0, 1],
        [0, 1, 1],
        [0, -1, -1],
        [0, 1, -1],
        [0, -1, 1],
    ]
)
CS = [tuple(int(c) for c in row) for row in lattice]
WEIGHT = [1.0 / 3.0] + [1.0 / 18.0] * 6 + [1.0 / 36.0] * 12
OPP = [0, 2, 1, 4, 3, 6, 5, 8, 7, 10, 9, 12, 11, 14, 13, 16, 15, 18, 17]
base_tau = 0.52
smag_coef = 0.04
speed_cap = 0.1
strain_floor = 1e-06
LIFTED = [k for k in range(19) if CS[k][2] != 0]


def tree_sum(items):
    items = list(items)
    while len(items) > 1:
        items = [items[i] + items[i + 1] if i + 1 < len(items) else items[i] for i in range(0, len(items), 2)]
    return items[0]


def peak_groups(ngx, ngy):
    if ngx * ngy <= 64:
        return [[(dx, dy) for dx in range(ngx) for dy in range(ngy) if dx or dy]]
    return [[(0, dy) for dy in range(1, ngy)], [(dx, 0) for dx in range(1, ngx)]]


def kernel(
    ngx, ngy,
    pops, heat_level, obstacle, table,
    out_p, out_v,
    st0, st1, rd, rho_s, v0, v1, hl, ob, tb, solid_s, pm_src, *rest,
):
    *pm_bufs, load_sem, a_send, a_recv, b_send, b_recv, p_send, p_recv = rest
    _, sx, sy, nz = pops.shape
    levels = table.shape[0]
    gx = lax.axis_index("gx")
    gy = lax.axis_index("gy")
    has_up = gy < ngy - 1
    has_down = gy > 0
    right = lax.rem(gx + 1, ngx)
    left = lax.rem(gx + ngx - 1, ngx)
    own_x = pl.ds(1, sx)
    own_y = pl.ds(ROW, sy)
    top = pl.ds(ROW + sy - 1, 1)
    bottom = pl.ds(ROW, 1)
    rim_low = pl.ds(ROW - 1, 1)
    rim_high = pl.ds(ROW + sy, 1)

    load_p = pltpu.make_async_copy(pops, st0.at[:, own_x, own_y, :], load_sem.at[0])
    load_h = pltpu.make_async_copy(heat_level, hl, load_sem.at[1])
    load_o = pltpu.make_async_copy(obstacle, ob, load_sem.at[2])
    load_p.start()
    load_h.start()
    load_o.start()
    load_t = pltpu.make_async_copy(table, tb, load_sem.at[3])
    load_t.start()

    barrier = pltpu.get_barrier_semaphore()

    def greet(x, y):
        pl.semaphore_signal(barrier, inc=1, device_id={"gx": x, "gy": y}, device_id_type=pl.DeviceIdType.MESH)

    groups = peak_groups(ngx, ngy)
    partners = sum(len(group) for group in groups)
    for group in groups:
        for dx, dy in group:
            greet(lax.rem(gx + dx, ngx), lax.rem(gy + dy, ngy))
    if len(groups) > 1:
        partners = partners + 2 * (jnp.where(has_up, 1, 0) + jnp.where(has_down, 1, 0))

        @pl.when(has_up)
        def _():
            greet(right, gy + 1)
            greet(left, gy + 1)

        @pl.when(has_down)
        def _():
            greet(right, gy - 1)
            greet(left, gy - 1)

    def zero_rim(rows):
        for ref in (st0, st1, v0, v1):
            ref[:, :, rows, :] = jnp.zeros((ref.shape[0], sx + 2, 1, nz), jnp.float32)

    @pl.when(jnp.logical_not(has_down))
    def _():
        zero_rim(rim_low)

    @pl.when(jnp.logical_not(has_up))
    def _():
        zero_rim(rim_high)

    sides = (
        (None, right, gy, (1, 0)),
        (None, left, gy, (-1, 0)),
        (has_up, gx, gy + 1, (0, 1)),
        (has_down, gx, gy - 1, (0, -1)),
        (has_up, right, gy + 1, (1, 1)),
        (has_down, left, gy - 1, (-1, -1)),
        (has_down, right, gy - 1, (1, -1)),
        (has_up, left, gy + 1, (-1, 1)),
    )
    arrives = (None, None, has_down, has_up, has_down, has_up, has_up, has_down)

    def src_dst(direction):
        dx, dy = direction
        xs = {1: (sx, 0), -1: (1, sx + 1), 0: (own_x, own_x)}[dx]
        ys = {1: (top, rim_low), -1: (bottom, rim_high), 0: (own_y, own_y)}[dy]
        return (xs[0], ys[0]), (xs[1], ys[1])

    def guarded(cond, fn):
        if cond is None:
            fn()
        else:
            pl.when(cond)(fn)

    def moving(direction):
        dx, dy = direction
        if dx and dy:
            return [k for k in range(19) if CS[k][:2] == direction]
        return [k for k in range(19) if (CS[k][0] == dx if dx else CS[k][1] == dy)]

    def exchange(ref, send, recv, many, groups):
        def start(number, x, y, direction):
            def go():
                s, d = src_dst(direction)
                for g in groups(direction):
                    pltpu.make_async_remote_copy(
                        src_ref=ref.at[g, s[0], s[1], :],
                        dst_ref=ref.at[g, d[0], d[1], :],
                        send_sem=send.at[number],
                        recv_sem=recv.at[number],
                        device_id={"gx": x, "gy": y},
                        device_id_type=pl.DeviceIdType.MESH,
                    ).start()
            return go

        for number, (cond, x, y, direction) in enumerate(sides[:many]):
            guarded(cond, start(number, x, y, direction))

        def total(number, direction, sem):
            def go():
                s, _ = src_dst(direction)
                gs = groups(direction)
                view = ref.at[pl.ds(0, len(gs)) if isinstance(gs[0], int) else gs[0], s[0], s[1], :]
                pltpu.make_async_copy(view, view, sem.at[number]).wait()
            return go

        def wait_recv():
            for number in range(many):
                guarded(arrives[number], total(number, sides[number][3], recv))

        def wait_send():
            for number in range(many):
                guarded(sides[number][0], total(number, sides[number][3], send))

        return wait_recv, wait_send

    def spread(step, phase, value):
        group = peak_groups(ngx, ngy)[phase]
        count = len(group)
        buf = pm_bufs[phase]
        pm_src[step, phase] = value
        for d, (dx, dy) in enumerate(group, 1):
            place = {"gx": lax.rem(gx + dx, ngx), "gy": lax.rem(gy + dy, ngy)}
            pltpu.make_async_remote_copy(
                src_ref=pm_src.at[step, phase],
                dst_ref=buf.at[step, d - 1],
                send_sem=p_send.at[step, phase],
                recv_sem=p_recv.at[step, phase],
                device_id=place,
                device_id_type=pl.DeviceIdType.MESH,
            ).start()

        def wait():
            pltpu.make_async_copy(buf.at[step], buf.at[step], p_recv.at[step, phase]).wait()
            best = value
            for d in range(count):
                best = jnp.maximum(best, buf[step, d])
            return best

        def wait_send():
            pltpu.make_async_copy(buf.at[step], buf.at[step], p_send.at[step, phase]).wait()

        return wait, wait_send

    blocks = [(x, r) for x in range(sx) for r in range(0, sy, ROW)]
    lane = lax.broadcasted_iota(jnp.int32, (ROW, nz), 1)
    first_lane = lane == 0
    last_lane = lane == nz - 1

    def streamed(st, fs):
        peak = jnp.zeros((ROW, nz), jnp.float32)
        vel = v0 if st is st0 else v1
        for x, r in blocks:
            reads = []
            for k, (cx, cy, cz) in enumerate(CS):
                rows = pl.ds(ROW + r - cy, ROW)
                cells = st[k, x + 1 - cx, rows, :]
                if cz:
                    if fs is not None:
                        cells = cells + (3.0 * WEIGHT[k] * cz) * (fs * v0[3, x + 1 - cx, rows, :])
                    cells = pltpu.roll(cells, cz % nz, 1)
                    cells = jnp.where(first_lane if cz > 0 else last_lane, 0.0, cells)
                rd[k, x, pl.ds(r, ROW), :] = cells
                reads.append(cells)
            density = tree_sum(reads)
            solid = solid_s[x, pl.ds(r, ROW), :] != 0
            inv = jnp.where(solid, 0.0, 1.0 / jnp.where(solid, 1.0, density))
            rho_s[x, pl.ds(r, ROW), :] = density
            speed = []
            for c in range(3):
                plus = tree_sum([reads[k] for k in range(19) if CS[k][c] > 0])
                minus = tree_sum([reads[k] for k in range(19) if CS[k][c] < 0])
                u = (plus - minus) * inv
                vel[c, x + 1, pl.ds(ROW + r, ROW), :] = u
                speed.append(u * u)
            peak = jnp.maximum(peak, speed[0] + speed[1] + speed[2])
        return peak

    def collided(vel, store):
        for x, r in blocks:
            mid = pl.ds(ROW + r, ROW)
            u = [vel[c, x + 1, mid, :] for c in range(3)]
            diff = []
            for a in range(3):
                diff.append(
                    (
                        vel[a, x + 2, mid, :] - vel[a, x, mid, :],
                        vel[a, x + 1, pl.ds(ROW + r + 1, ROW), :] - vel[a, x + 1, pl.ds(ROW + r - 1, ROW), :],
                        pltpu.roll(u[a], nz - 1, 1) - pltpu.roll(u[a], 1, 1),
                    )
                )
            own = diff[0][0] * diff[0][0] + diff[1][1] * diff[1][1] + diff[2][2] * diff[2][2]
            xy = diff[0][1] + diff[1][0]
            xz = diff[0][2] + diff[2][0]
            yz = diff[1][2] + diff[2][1]
            size = jnp.sqrt(0.5 * own + 0.25 * (xy * xy + xz * xz + yz * yz) + strain_floor)
            omega = 1.0 / (base_tau + 3.0 * smag_coef * size)
            solid = solid_s[x, pl.ds(r, ROW), :] != 0
            density = rho_s[x, pl.ds(r, ROW), :]
            still = 1.0 - 1.5 * (u[0] * u[0] + u[1] * u[1] + u[2] * u[2])
            reads = [rd[k, x, pl.ds(r, ROW), :] for k in range(19)]
            scaled = {w: (w * density) * omega for w in sorted(set(WEIGHT))}
            keep = 1.0 - omega
            store(0, x, r, jnp.where(solid, reads[0], keep * reads[0] + scaled[WEIGHT[0]] * still))
            for k in range(1, 19, 2):
                other = OPP[k]
                project = None
                for c in range(3):
                    if CS[k][c]:
                        if project is None:
                            project = u[c] if CS[k][c] > 0 else -u[c]
                        else:
                            project = project + u[c] if CS[k][c] > 0 else project - u[c]
                even = still + 4.5 * project * project
                odd = 3.0 * project
                weight = scaled[WEIGHT[k]]
                store(k, x, r, jnp.where(solid, reads[other], keep * reads[k] + weight * (even + odd)))
                store(other, x, r, jnp.where(solid, reads[k], keep * reads[other] + weight * (even - odd)))

    def scale_of(tile):
        peak = jnp.max(jnp.max(tile, axis=0, keepdims=True), axis=1, keepdims=True)
        peak = jnp.broadcast_to(peak, (ROW, nz))
        return speed_cap / jnp.sqrt(speed_cap * speed_cap + peak)

    gone = []

    load_p.wait()
    pl.semaphore_wait(barrier, partners)
    wait_a, sent = exchange(st0, a_send.at[0], a_recv.at[0], 8, moving)
    gone.append(sent)
    load_h.wait()
    load_o.wait()
    load_t.wait()
    for x, r in blocks:
        rows = pl.ds(r, ROW)
        code = hl[x, rows, :]
        heat = jnp.zeros((ROW, nz), jnp.float32)
        for level in range(levels):
            heat = jnp.where(code == level, tb[level], heat)
        grid_y = gy * sy + r + lax.broadcasted_iota(jnp.int32, (ROW, nz), 0)
        solid = (
            (ob[x, rows, :] == 1) | (grid_y == 0) | (grid_y == ngy * sy - 1) | first_lane | last_lane
        )
        solid_s[x, rows, :] = jnp.where(solid, 1, 0)
        v0[3, x + 1, pl.ds(ROW + r, ROW), :] = jnp.where(solid, 0.0, heat)
    wait_a()
    peak = streamed(st0, None)

    wait_b, sent = exchange(v0, b_send.at[0], b_recv.at[0], 4, lambda direction: [pl.ds(0, 4)])
    gone.append(sent)
    wait_peak, sent = spread(0, 0, peak)
    gone.append(sent)
    wait_b()
    for phase in range(1, len(pm_bufs)):
        wait_peak, sent = spread(0, phase, wait_peak())
        gone.append(sent)

    def store_st1(k, x, r, value):
        st1[k, x + 1, pl.ds(ROW + r, ROW), :] = value

    collided(v0, store_st1)

    wait_a, sent = exchange(st1, a_send.at[1], a_recv.at[1], 8, moving)
    gone.append(sent)
    fs = scale_of(wait_peak())
    wait_a()
    peak = streamed(st1, fs)

    wait_b, sent = exchange(v1, b_send.at[1], b_recv.at[1], 4, lambda direction: [pl.ds(0, 3)])
    gone.append(sent)
    wait_peak, sent = spread(1, 0, peak)
    gone.append(sent)
    for x, r in blocks:
        for c in range(3):
            out_v[c, x, pl.ds(r, ROW), :] = v1[c, x + 1, pl.ds(ROW + r, ROW), :]
    wait_b()
    for phase in range(1, len(pm_bufs)):
        wait_peak, sent = spread(1, phase, wait_peak())
        gone.append(sent)

    def store_out(k, x, r, value):
        out_p[k, x, pl.ds(r, ROW), :] = value

    collided(v1, store_out)
    fs = scale_of(wait_peak())
    lift = {(x, r): fs * v0[3, x + 1, pl.ds(ROW + r, ROW), :] for x, r in blocks}
    for k in LIFTED:
        for x, r in blocks:
            rows = pl.ds(r, ROW)
            out_p[k, x, rows, :] = out_p[k, x, rows, :] + (3.0 * WEIGHT[k] * CS[k][2]) * lift[(x, r)]
    for sent in gone:
        sent()


def write_out(pops, vel, out_p, out_v, sems):
    copies = [
        pltpu.make_async_copy(pops, out_p, sems.at[0]),
        pltpu.make_async_copy(vel, out_v, sems.at[1]),
    ]
    for copy in copies:
        copy.start()
    for copy in copies:
        copy.wait()


def local(populations, heat_level, obstacle, heat_table):
    ngx = lax.axis_size("gx")
    ngy = lax.axis_size("gy")
    _, sx, sy, nz = populations.shape
    f32 = jnp.float32
    wide = (sx + 2, sy + 2 * ROW, nz)
    dma = pltpu.SemaphoreType.DMA
    groups = peak_groups(ngx, ngy)
    phases = len(groups)
    vmem = pl.BlockSpec(memory_space=pltpu.VMEM)
    anywhere = pl.BlockSpec(memory_space=pltpu.HBM)
    shapes = (
        jax.ShapeDtypeStruct(populations.shape, f32),
        jax.ShapeDtypeStruct((3, sx, sy, nz), f32),
    )
    pops, velocity = pl.pallas_call(
        functools.partial(kernel, ngx, ngy),
        out_shape=shapes,
        in_specs=[anywhere] * 4,
        out_specs=[vmem] * 2,
        scratch_shapes=[
            pltpu.VMEM((19,) + wide, f32),
            pltpu.VMEM((19,) + wide, f32),
            pltpu.VMEM((19, sx, sy, nz), f32),
            pltpu.VMEM((sx, sy, nz), f32),
            pltpu.VMEM((4,) + wide, f32),
            pltpu.VMEM((3,) + wide, f32),
            pltpu.VMEM((sx, sy, nz), jnp.int32),
            pltpu.VMEM((sx, sy, nz), jnp.int32),
            pltpu.SMEM(heat_table.shape, f32),
            pltpu.VMEM((sx, sy, nz), jnp.int32),
            pltpu.VMEM((STEPS, phases, ROW, nz), f32),
            *[pltpu.VMEM((STEPS, len(group), ROW, nz), f32) for group in groups],
            dma((4,)),
            dma((STEPS, 8)),
            dma((STEPS, 8)),
            dma((STEPS, 4)),
            dma((STEPS, 4)),
            dma((STEPS, phases)),
            dma((STEPS, phases)),
        ],
        compiler_params=pltpu.CompilerParams(
            collective_id=0, has_side_effects=True, vmem_limit_bytes=24 * 1024 * 1024
        ),
        name="lattice_steps",
    )(*[pltpu.with_memory_space_constraint(a, pltpu.HBM) for a in (populations, heat_level, obstacle, heat_table)])
    return pl.pallas_call(
        write_out,
        out_shape=shapes,
        in_specs=[vmem] * 2,
        out_specs=[anywhere] * 2,
        scratch_shapes=[dma((2,))],
        compiler_params=pltpu.CompilerParams(vmem_limit_bytes=8 * 1024 * 1024),
        name="write_out",
    )(pops, velocity)


def solution(mesh):
    return jax.shard_map(
        local,
        mesh=mesh,
        in_specs=(
            P(None, ("member", "gx"), "gy", None),
            P(("member", "gx"), "gy", None),
            P(("member", "gx"), "gy", None),
            P(),
        ),
        out_specs=(P(None, ("member", "gx"), "gy", None), P(None, ("member", "gx"), "gy", None)),
        check_vma=False,
    )
```

profile of v0, /device:TPU:0, one launch (start us, length us, event | category | flops | bytes accessed | tf_op | source)
XLA Modules:
  0.0 26.9 jit_solution(17492955169397434608)
XLA Ops:
  0.6 25.4 %lattice_steps.1 = (f32[19,4,16,128]{3,2,1,0:T(8,128)S(1)}, f32[3,4,16,128]{3,2,1,0:T(8,128)S(1)}) custom-call(f32[19,4,16,128]{3,2,1,0:T(8,128)} %pops.1, s32[4,16,128]{2,1,0:T(8,128)} %heat_level.1, s32[4,16,128]{2,1,0:T(8,128)} %obstacle.1, f32[8]{0:T(128)} %table.1), custom_call_target="tpu_custom_call" | custom-call | tf_op jit(solution)/shard_map/lattice_steps/pallas_call | solution.py:396
  26.0 0.9 %write_out.1 = (f32[19,4,16,128]{3,2,1,0:T(8,128)}, f32[3,4,16,128]{3,2,1,0:T(8,128)}) custom-call(f32[19,4,16,128]{3,2,1,0:T(8,128)S(1)} %get-tuple-element.4.pops, f32[3,4,16,128]{3,2,1,0:T(8,128)S(1)} %get-tuple-element.5.vel), custom_call_target="tpu_custom_call" | custom-call | tf_op jit(solution)/shard_map/write_out/pallas_call | solution.py:427
where the time goes:
time: 27 us; the launch traced here: 26.9 us
  Pallas kernels  26.2 us (97%)
  between operations  0.64 us (2%)
    pallas_call x1, Pallas kernels, local(): pl.pallas_call(functools.partial(kernel, ngx, ngy), out_shape=shapes, in_...  25.4 us
    pallas_call x1, Pallas kernels, local(): pl.pallas_call(write_out, out_shape=shapes, in_specs=[vmem] * 2, out_spec...  0.87 us

commit v1 on v0

v1 whole, which is shorter than its diff:
```python
import functools

import jax
import jax.numpy as jnp
import numpy as np
from jax import lax
from jax.experimental import pallas as pl
from jax.experimental.pallas import tpu as pltpu
from jax.sharding import PartitionSpec as P

STEPS = 2
ROW = 8

lattice = np.array(
    [
        [0, 0, 0],
        [1, 0, 0],
        [-1, 0, 0],
        [0, 1, 0],
        [0, -1, 0],
        [0, 0, 1],
        [0, 0, -1],
        [1, 1, 0],
        [-1, -1, 0],
        [1, -1, 0],
        [-1, 1, 0],
        [1, 0, 1],
        [-1, 0, -1],
        [1, 0, -1],
        [-1, 0, 1],
        [0, 1, 1],
        [0, -1, -1],
        [0, 1, -1],
        [0, -1, 1],
    ]
)
CS = [tuple(int(c) for c in row) for row in lattice]
NUMBER = {c: k for k, c in enumerate(CS)}
WEIGHT = [1.0 / 3.0] + [1.0 / 18.0] * 6 + [1.0 / 36.0] * 12
OPP = [0, 2, 1, 4, 3, 6, 5, 8, 7, 10, 9, 12, 11, 14, 13, 16, 15, 18, 17]
base_tau = 0.52
smag_coef = 0.04
speed_cap = 0.1
strain_floor = 1e-06
LIFTED = [k for k in range(19) if CS[k][2] != 0]
ACROSS_X = {c: [NUMBER[(c, 0, 0)], NUMBER[(c, 1, 0)], NUMBER[(c, -1, 0)], NUMBER[(c, 0, 1)], NUMBER[(c, 0, -1)]] for c in (1, -1)}
ACROSS_Y = {c: [NUMBER[(0, c, 0)], NUMBER[(1, c, 0)], NUMBER[(-1, c, 0)], NUMBER[(0, c, 1)], NUMBER[(0, c, -1)]] for c in (1, -1)}
OUT = (-1, 1)
IN = (1, -1)


def tree_sum(items):
    items = list(items)
    while len(items) > 1:
        items = [items[i] + items[i + 1] if i + 1 < len(items) else items[i] for i in range(0, len(items), 2)]
    return items[0]


def peak_groups(ngx, ngy):
    if ngx * ngy <= 64:
        return [[(dx, dy) for dx in range(ngx) for dy in range(ngy) if dx or dy]]
    return [[(0, dy) for dy in range(1, ngy)], [(dx, 0) for dx in range(1, ngx)]]


def kernel(
    ngx, ngy,
    pops, heat_level, obstacle, table,
    out_p, out_v,
    st0, st1, rd, ms, rho_s, vel, hl, ob, tb, solid_s,
    hb, hzp, hzm, hm, hmy,
    xr, xm_out, xm_in, yb_out, yb_in, cg, cm_out, cr_in, cm_in,
    ox, oy, dr, dm, tu, ex, ey, gfx, gfy, pm_src, *rest,
):
    (*pm_bufs, load_sem, xr_send, xr_recv, xm_send, xm_recv, yr_send, yr_recv, ym_send, ym_recv,
     cr_send, cr_recv, cm_send, cm_recv, h_send, h_recv, p_send, p_recv) = rest
    _, sx, sy, nz = pops.shape
    levels = table.shape[0]
    gx = lax.axis_index("gx")
    gy = lax.axis_index("gy")
    has_up = gy < ngy - 1
    has_down = gy > 0
    right = lax.rem(gx + 1, ngx)
    left = lax.rem(gx + ngx - 1, ngx)
    own_y = pl.ds(ROW, sy)
    face_x = (0, sx - 1)
    edge_y = (0, sy - 1)
    x_of = (left, right)
    y_of = (gy - 1, gy + 1)
    has_y = (has_down, has_up)

    load_p = pltpu.make_async_copy(pops, st0.at[:, :, own_y, :], load_sem.at[0])
    load_h = pltpu.make_async_copy(heat_level, hl, load_sem.at[1])
    load_o = pltpu.make_async_copy(obstacle, ob, load_sem.at[2])
    load_p.start()
    load_h.start()
    load_o.start()
    load_t = pltpu.make_async_copy(table, tb, load_sem.at[3])
    load_t.start()

    barrier = pltpu.get_barrier_semaphore()

    def greet(x, y):
        pl.semaphore_signal(barrier, inc=1, device_id={"gx": x, "gy": y}, device_id_type=pl.DeviceIdType.MESH)

    groups = peak_groups(ngx, ngy)
    partners = sum(len(group) for group in groups)
    for group in groups:
        for dx, dy in group:
            greet(lax.rem(gx + dx, ngx), lax.rem(gy + dy, ngy))
    if len(groups) > 1:
        partners = partners + 2 * (jnp.where(has_up, 1, 0) + jnp.where(has_down, 1, 0))
        for s in (0, 1):

            @pl.when(has_y[s])
            def _():
                greet(right, y_of[s])
                greet(left, y_of[s])

    def zeros(ref, *index):
        part = ref.at[index]
        part[...] = jnp.zeros(part.shape, jnp.float32)

    every = slice(None)
    for row in (ROW - 1, ROW + sy):
        for st in (st0, st1):
            for c in (1, -1):
                for k in ACROSS_Y[c]:
                    zeros(st, k, every, pl.ds(row, 1), every)
        zeros(xr, every, every, every, pl.ds(row, 1), every)
    for ref in (cg, tu, ey):
        ref[...] = jnp.zeros(ref.shape, jnp.float32)

    for s in (0, 1):

        @pl.when(jnp.logical_not(has_y[s]))
        def _():
            zeros(yb_in, every, every, pl.ds(s * sx, sx), every)
            for xs in (0, 1):
                zeros(cr_in, every, pl.ds(xs * 2 + s, 1), every)
                zeros(cm_in, every, every, pl.ds(xs * 2 + s, 1), every)
            zeros(hb, every, pl.ds((ROW - 2, ROW + sy)[s], 2), every)

    gone = []

    def guarded(cond, fn):
        if cond is None:
            fn()
        else:
            pl.when(cond)(fn)

    def send(cond, pairs, send_sem, recv_sem, x, y):
        def go():
            for src, dst in pairs:
                pltpu.make_async_remote_copy(
                    src_ref=src, dst_ref=dst, send_sem=send_sem, recv_sem=recv_sem,
                    device_id={"gx": x, "gy": y}, device_id_type=pl.DeviceIdType.MESH,
                ).start()

        guarded(cond, go)

    def await_bytes(cond, view, sem):
        guarded(cond, lambda: pltpu.make_async_copy(view, view, sem).wait())

    def send_later(cond, view, sem):
        gone.append(lambda: await_bytes(cond, view, sem))

    states = (st0, st1)

    def x_raw(step, s):
        st = states[step]
        return [(st.at[k, face_x[s], own_y, :], xr.at[step, 1 - s, j, own_y, :]) for j, k in enumerate(ACROSS_X[OUT[s]])]

    def send_x_raw(step):
        def go(s):
            send(None, x_raw(step, s), xr_send.at[step, s], xr_recv.at[step, 1 - s], x_of[s], gy)

        @pl.when(gx == 0)
        def _():
            go(0)
            go(1)

        @pl.when(gx != 0)
        def _():
            go(1)
            go(0)

        for s in (0, 1):
            send_later(None, states[step].at[pl.ds(0, 5), 0, own_y, :], xr_send.at[step, s])

    def send_x_sums(step):
        def go(s):
            send(None, [(xm_out.at[step, s], xm_in.at[step, 1 - s])], xm_send.at[step, s], xm_recv.at[step, 1 - s], x_of[s], gy)

        @pl.when(gx == 0)
        def _():
            go(0)
            go(1)

        @pl.when(gx != 0)
        def _():
            go(1)
            go(0)

        for s in (0, 1):
            send_later(None, xm_out.at[step, s], xm_send.at[step, s])

    def send_y(step, fields, send_sem, recv_sem):
        for s in (0, 1):
            src = yb_out.at[step, fields, pl.ds(s * sx, sx), :]
            dst = yb_in.at[step, fields, pl.ds((1 - s) * sx, sx), :]
            send(has_y[s], [(src, dst)], send_sem.at[step, s], recv_sem.at[step, 1 - s], gx, y_of[s])
            send_later(has_y[s], src, send_sem.at[step, s])

    corners = [(xs, ys) for xs in (0, 1) for ys in (0, 1)]

    def send_corner_raw(step):
        st = states[step]
        for c, (xs, ys) in enumerate(corners):
            k = NUMBER[(OUT[xs], OUT[ys], 0)]
            src = st.at[k, face_x[xs], pl.ds(ROW + edge_y[ys], 1), :]
            send(has_y[ys], [(src, cr_in.at[step, pl.ds(3 - c, 1), :])], cr_send.at[step, c], cr_recv.at[step, 3 - c], x_of[xs], y_of[ys])
            send_later(has_y[ys], src, cr_send.at[step, c])

    def send_corner_sums(step):
        for c, (xs, ys) in enumerate(corners):
            src = cm_out.at[step, :, pl.ds(c, 1), :]
            send(has_y[ys], [(src, cm_in.at[step, :, pl.ds(3 - c, 1), :])], cm_send.at[step, c], cm_recv.at[step, 3 - c], x_of[xs], y_of[ys])
            send_later(has_y[ys], src, cm_send.at[step, c])

    def await_raw(step):
        for s in (0, 1):
            await_bytes(has_y[s], yb_in.at[step, pl.ds(0, 5), pl.ds(s * sx, sx), :], yr_recv.at[step, s])
        for c, (xs, ys) in enumerate(corners):
            await_bytes(has_y[ys], cr_in.at[step, pl.ds(c, 1), :], cr_recv.at[step, c])
        for s in (0, 1):
            await_bytes(None, xr.at[step, s, :, own_y, :], xr_recv.at[step, s])

    def await_sums(step):
        for s in (0, 1):
            await_bytes(has_y[s], yb_in.at[step, pl.ds(5, 4), pl.ds(s * sx, sx), :], ym_recv.at[step, s])
        for c, (xs, ys) in enumerate(corners):
            await_bytes(has_y[ys], cm_in.at[step, :, pl.ds(c, 1), :], cm_recv.at[step, c])
        for s in (0, 1):
            await_bytes(None, xm_in.at[step, s], xm_recv.at[step, s])

    raw_fields = pl.ds(0, 5)
    sum_fields = pl.ds(5, 4)

    def heat_moves():
        moves = []
        layers = ((2, sx), (0, sx + 2))
        for s in (0, 1):
            src = hb.at[pl.ds(layers[0][s], 2), own_y, :]
            dst = hb.at[pl.ds((sx + 2, 0)[s], 2), own_y, :]
            moves.append((None, src, dst, x_of[s], gy))
        for s in (0, 1):
            src = hb.at[pl.ds(2, sx), pl.ds((ROW, ROW + sy - 2)[s], 2), :]
            dst = hb.at[pl.ds(2, sx), pl.ds((ROW + sy, ROW - 2)[s], 2), :]
            moves.append((has_y[s], src, dst, gx, y_of[s]))
        for xs, ys in corners:
            src = hb.at[2 + face_x[xs], pl.ds(ROW + edge_y[ys], 1), :]
            dst = hb.at[(sx + 2, 1)[xs], pl.ds((ROW + sy, ROW - 1)[ys], 1), :]
            moves.append((has_y[ys], src, dst, x_of[xs], y_of[ys]))
        return moves

    arrives_on = (1, 0, 3, 2, 7, 6, 5, 4)

    def send_heat():
        for number, (cond, src, dst, x, y) in enumerate(heat_moves()):
            send(cond, [(src, dst)], h_send.at[number], h_recv.at[number], x, y)
            send_later(cond, src, h_send.at[number])

    def await_heat():
        moves = heat_moves()
        for number, (_, src, dst, _, _) in enumerate(moves):
            await_bytes(moves[arrives_on[number]][0], dst, h_recv.at[number])

    def spread(step, phase, value):
        group = peak_groups(ngx, ngy)[phase]
        count = len(group)
        buf = pm_bufs[phase]
        pm_src[step, phase] = value
        for d, (dx, dy) in enumerate(group, 1):
            place = {"gx": lax.rem(gx + dx, ngx), "gy": lax.rem(gy + dy, ngy)}
            pltpu.make_async_remote_copy(
                src_ref=pm_src.at[step, phase],
                dst_ref=buf.at[step, pl.ds(d - 1, 1), :],
                send_sem=p_send.at[step, phase],
                recv_sem=p_recv.at[step, phase],
                device_id=place,
                device_id_type=pl.DeviceIdType.MESH,
            ).start()
        view = buf.at[step, pl.ds(0, count), :]
        send_later(None, view, p_send.at[step, phase])

        def wait():
            await_bytes(None, view, p_recv.at[step, phase])
            return jnp.maximum(value, jnp.max(buf[step, pl.ds(0, count), :], axis=0, keepdims=True))

        return wait

    def spread_all(step, tile):
        wait = spread(step, 0, jnp.max(tile, axis=0, keepdims=True))

        def finish():
            best = wait()
            for phase in range(1, len(pm_bufs)):
                best = spread(step, phase, best)()
            peak = jnp.broadcast_to(jnp.max(best, axis=1, keepdims=True), (ROW, nz))
            return speed_cap / jnp.sqrt(speed_cap * speed_cap + peak)

        return finish

    blocks = [(x, r) for x in range(sx) for r in range(0, sy, ROW)]
    outer = [(x, r) for x, r in blocks if x in face_x]
    inner = [(x, r) for x, r in blocks if x not in face_x]
    lane = lax.broadcasted_iota(jnp.int32, (ROW, nz), 1)
    row_no = lax.broadcasted_iota(jnp.int32, (ROW, nz), 0)
    first_lane = lane == 0
    last_lane = lane == nz - 1
    edge_row = (row_no == 0, row_no == ROW - 1)
    pack_row = lax.broadcasted_iota(jnp.int32, (2 * sx, nz), 0)
    pack_sign = jnp.where(pack_row < sx, 1.0, -1.0)
    corner_x = jnp.where(row_no < 2, 1.0, -1.0)
    corner_y = jnp.where(lax.rem(row_no, 2) == 0, 1.0, -1.0)

    def shift_z(cells, cz):
        if not cz:
            return cells
        at = lax.broadcasted_iota(jnp.int32, cells.shape, 1)
        return jnp.where(at == (0 if cz > 0 else nz - 1), 0.0, pltpu.roll(cells, cz % nz, 1))

    def edges_of(r):
        return [s for s in (0, 1) if r == (0, sy - ROW)[s]]

    def own_sums(step, tiles):
        st = states[step]
        for x, r in tiles:
            rows = pl.ds(r, ROW)
            reads = {}
            for k, (cx, cy, cz) in enumerate(CS):
                if 0 <= x - cx < sx:
                    reads[k] = shift_z(st[k, x - cx, pl.ds(ROW + r - cy, ROW), :], cz)
                    rd[k, x, rows, :] = reads[k]
            sums = [tree_sum(list(reads.values()))]
            for c in range(3):
                plus = [reads[k] for k in reads if CS[k][c] > 0]
                minus = [reads[k] for k in reads if CS[k][c] < 0]
                if plus and minus:
                    sums.append(tree_sum(plus) - tree_sum(minus))
                else:
                    sums.append(tree_sum(plus) if plus else -tree_sum(minus))
            for m in range(4):
                ms[m, x, rows, :] = sums[m]
            sums[0] = jnp.where(solid_s[x, rows, :] != 0, 0.0, sums[0])
            for s in (0, 1):
                if x == face_x[s]:
                    for m in range(4):
                        xm_out[step, s, m, rows, :] = sums[m]
                if s in edges_of(r):
                    at = (0, ROW - 1)[s]
                    for m in range(4):
                        yb_out[step, 5 + m, pl.ds(s * sx + x, 1), :] = sums[m][at : at + 1, :]

    def pack_y_raw(step):
        st = states[step]
        for s in (0, 1):
            for j, k in enumerate(ACROSS_Y[OUT[s]]):
                for x in range(sx):
                    yb_out[step, j, pl.ds(s * sx + x, 1), :] = st[k, x, pl.ds(ROW + edge_y[s], 1), :]

    def corner_sums(step):
        st = states[step]
        for c, (xs, ys) in enumerate(corners):
            dx, dy = OUT[xs], OUT[ys]
            fx, fy = face_x[xs], edge_y[ys]
            places = [
                ((0, dy, 0), fx, fy), ((0, dy, 1), fx, fy), ((0, dy, -1), fx, fy), ((dx, dy, 0), fx - dx, fy),
                ((dx, 0, 0), fx, fy), ((dx, 0, 1), fx, fy), ((dx, 0, -1), fx, fy), ((dx, dy, 0), fx, fy - dy),
            ]
            for f, (direction, x, y) in enumerate(places):
                cg[f, pl.ds(c, 1), :] = st[NUMBER[direction], x, pl.ds(ROW + y, 1), :]
        for half, sign in ((0, -corner_x), (1, -corner_y)):
            a, b, d, e = (cg[4 * half + f] for f in range(4))
            b, d = shift_z(b, 1), shift_z(d, -1)
            cm_out[step, 3 * half + 0] = (a + b) + (d + e)
            cm_out[step, 3 * half + 1] = sign * e
            cm_out[step, 3 * half + 2] = b - d

    def packed(fields, fill):
        plus = jnp.where(lax.rem(pack_row, sx) == 0, 0.0, pltpu.roll(fields[1], 1, 0))
        minus = jnp.where(lax.rem(pack_row, sx) == sx - 1, 0.0, pltpu.roll(fields[2], 2 * sx - 1, 0))
        if fill is not None:
            for ys in (0, 1):
                plus = jnp.where(pack_row == ys * sx, fill(ys), plus)
                minus = jnp.where(pack_row == ys * sx + sx - 1, fill(2 + ys), minus)
        return [fields[0], plus, minus, shift_z(fields[3], 1), shift_z(fields[4], -1)]

    def ghost_shares(step):
        st = states[step]
        for s in (0, 1):
            for r in range(0, sy, ROW):
                ks = ACROSS_X[OUT[s]]
                a, b, c, d, e = (st[k, face_x[s], pl.ds(ROW + r - CS[k][1], ROW), :] for k in ks)
                d, e = shift_z(d, 1), shift_z(e, -1)
                ox[s, 0, pl.ds(r, ROW), :] = ((a + b) + (c + d)) + e
                ox[s, 1, pl.ds(r, ROW), :] = b - c
                ox[s, 2, pl.ds(r, ROW), :] = d - e
        a, b, c, d, e = packed([yb_out[step, j] for j in range(5)], None)
        total = ((a + b) + (c + d)) + e
        oy[0] = total
        oy[1] = b - c
        oy[2] = -pack_sign * total
        oy[3] = d - e

    def velocity_pass(step, fs):
        fields = packed([yb_in[step, j] for j in range(5)], lambda c: cr_in[step, pl.ds(c, 1), :])
        for j in range(5):
            dr[j] = fields[j]
        a, b, c, d, e = fields
        total = ((a + b) + (c + d)) + e
        for m, value in enumerate((total, b - c, pack_sign * total, d - e)):
            dm[m] = value
        peak = jnp.zeros((ROW, nz), jnp.float32)
        for x, r in blocks:
            rows = pl.ds(r, ROW)
            sums = [ms[m, x, rows, :] for m in range(4)]
            for s in (0, 1):
                if x == face_x[s]:
                    ks = ACROSS_X[IN[s]]
                    parts = [
                        shift_z(xr[step, s, j, pl.ds(ROW + r - CS[k][1], ROW), :], CS[k][2]) for j, k in enumerate(ks)
                    ]
                    for k, part in zip(ks, parts):
                        rd[k, x, rows, :] = part
                    share = tree_sum(parts)
                    sums[0] = sums[0] + share
                    sums[1] = sums[1] + share if s == 0 else sums[1] - share
                    sums[2] = sums[2] + (parts[1] - parts[2])
                    sums[3] = sums[3] + (parts[3] - parts[4])
            for s in edges_of(r):
                for m in range(4):
                    sums[m] = sums[m] + jnp.where(edge_row[s], dm[m, pl.ds(s * sx + x, 1), :], 0.0)
            if fs is not None:
                sums = [sums[m] + fs * hm[m, x + 1, rows, :] for m in range(4)]
            solid = solid_s[x, rows, :] != 0
            inv = jnp.where(solid, 0.0, 1.0 / jnp.where(solid, 1.0, sums[0]))
            rho_s[x, rows, :] = sums[0]
            speed = []
            for c in range(3):
                u = sums[1 + c] * inv
                vel[c, x + 1, pl.ds(ROW + r, ROW), :] = u
                speed.append(u * u)
            peak = jnp.maximum(peak, speed[0] + speed[1] + speed[2])
        return peak

    def edge_reads():
        for s in (0, 1):
            for j, k in enumerate(ACROSS_Y[IN[s]]):
                for x in range(sx):
                    rd[k, x, pl.ds(edge_y[s], 1), :] = dr[j, pl.ds(s * sx + x, 1), :]

    def ghost_pass(step, fs):
        for c, (xs, ys) in enumerate(corners):
            j = 1 if OUT[xs] > 0 else 2
            tu[0, pl.ds(c, 1), :] = yb_in[step, j, pl.ds(ys * sx + face_x[xs], 1), :]
            j = 1 if OUT[ys] > 0 else 2
            tu[1, pl.ds(c, 1), :] = xr[step, xs, j, pl.ds(ROW + edge_y[ys], 1), :]
        over, up = tu[0], tu[1]
        total = cm_in[step, 0] + over
        for m, value in enumerate((total, cm_in[step, 1] - corner_x * over, corner_y * total, cm_in[step, 2])):
            ex[m] = value
        total = cm_in[step, 3] + up
        for m, value in enumerate((total, corner_x * total, cm_in[step, 4] - corner_y * up, cm_in[step, 5])):
            for c, (xs, ys) in enumerate(corners):
                ey[m, pl.ds(ys * sx + face_x[xs], 1), :] = value[c : c + 1, :]
        for s in (0, 1):
            for r in range(0, sy, ROW):
                rows = pl.ds(r, ROW)
                share = ox[s, 0, rows, :]
                sums = [xm_in[step, s, m, rows, :] for m in range(4)]
                if step == 0:
                    gfx[s, rows, :] = sums[0]
                fluid = gfx[s, rows, :] > 0.0
                sums[0] = sums[0] + share
                sums[1] = sums[1] - share if s == 0 else sums[1] + share
                sums[2] = sums[2] + ox[s, 1, rows, :]
                sums[3] = sums[3] + ox[s, 2, rows, :]
                for ys in edges_of(r):
                    for m in range(4):
                        sums[m] = sums[m] + jnp.where(edge_row[ys], ex[m, pl.ds(s * 2 + ys, 1), :], 0.0)
                at = (0, sx + 1)[s]
                if fs is not None:
                    sums = [sums[m] + fs * hm[m, at, rows, :] for m in range(4)]
                inv = jnp.where(fluid, 1.0 / jnp.where(fluid, sums[0], 1.0), 0.0)
                for c in range(3):
                    vel[c, at, pl.ds(ROW + r, ROW), :] = sums[1 + c] * inv
        sums = [yb_in[step, 5 + m] for m in range(4)]
        if step == 0:
            gfy[...] = sums[0]
        fluid = gfy[...] > 0.0
        sums = [sums[m] + oy[m] + ey[m] for m in range(4)]
        if fs is not None:
            sums = [sums[m] + fs[0:1, :] * hmy[m] for m in range(4)]
        inv = jnp.where(fluid, 1.0 / jnp.where(fluid, sums[0], 1.0), 0.0)
        for c in range(3):
            u = sums[1 + c] * inv
            for s in (0, 1):
                for x in range(sx):
                    at = s * sx + x
                    vel[c, x + 1, pl.ds((ROW - 1, ROW + sy)[s], 1), :] = u[at : at + 1, :]

    def heat_sums():
        for x in range(sx + 4):
            spans = [(ROW + r, ROW) for r in range(0, sy, ROW)]
            if 1 <= x <= sx + 2:
                spans += [(ROW - 2, 2), (ROW + sy, 2)]
            for at, span in spans:
                if span != ROW and x in (1, sx + 2):
                    at, span = (at + 1, 1) if at < ROW else (at, 1)
                cells = hb[x, pl.ds(at, span), :]
                hzp[x, pl.ds(at, span), :] = shift_z(cells, 1)
                hzm[x, pl.ds(at, span), :] = shift_z(cells, -1)

        def at(x, row, span):
            cells = [
                (hzp[i, pl.ds(y, span), :], hzm[i, pl.ds(y, span), :])
                for i, y in ((x, row), (x - 1, row), (x + 1, row), (x, row - 1), (x, row + 1))
            ]
            diff = [a - b for a, b in cells]
            both = [a + b for a, b in cells]
            main, side = 3.0 * WEIGHT[5], 3.0 * WEIGHT[11]
            return (
                main * diff[0] + side * ((diff[1] + diff[2]) + (diff[3] + diff[4])),
                side * (diff[1] - diff[2]),
                side * (diff[3] - diff[4]),
                main * both[0] + side * ((both[1] + both[2]) + (both[3] + both[4])),
            )

        for x in range(sx + 2):
            for r in range(0, sy, ROW):
                for m, value in enumerate(at(x + 1, ROW + r, ROW)):
                    hm[m, x, pl.ds(r, ROW), :] = value
        for s in (0, 1):
            for x in range(sx):
                for m, value in enumerate(at(x + 2, (ROW - 1, ROW + sy)[s], 1)):
                    hmy[m, pl.ds(s * sx + x, 1), :] = value

    def collided(tiles, fs, store):
        for x, r in tiles:
            mid = pl.ds(ROW + r, ROW)
            u = [vel[c, x + 1, mid, :] for c in range(3)]
            diff = []
            for a in range(3):
                diff.append(
                    (
                        vel[a, x + 2, mid, :] - vel[a, x, mid, :],
                        vel[a, x + 1, pl.ds(ROW + r + 1, ROW), :] - vel[a, x + 1, pl.ds(ROW + r - 1, ROW), :],
                        pltpu.roll(u[a], nz - 1, 1) - pltpu.roll(u[a], 1, 1),
                    )
                )
            own = diff[0][0] * diff[0][0] + diff[1][1] * diff[1][1] + diff[2][2] * diff[2][2]
            xy = diff[0][1] + diff[1][0]
            xz = diff[0][2] + diff[2][0]
            yz = diff[1][2] + diff[2][1]
            size = jnp.sqrt(0.5 * own + 0.25 * (xy * xy + xz * xz + yz * yz) + strain_floor)
            omega = 1.0 / (base_tau + 3.0 * smag_coef * size)
            solid = solid_s[x, pl.ds(r, ROW), :] != 0
            density = rho_s[x, pl.ds(r, ROW), :]
            still = 1.0 - 1.5 * (u[0] * u[0] + u[1] * u[1] + u[2] * u[2])
            reads = [rd[k, x, pl.ds(r, ROW), :] for k in range(19)]
            if fs is not None:
                for k in LIFTED:
                    cx, cy, cz = CS[k]
                    source = hzp if cz > 0 else hzm
                    reads[k] = reads[k] + (3.0 * WEIGHT[k] * cz) * (fs * source[x + 2 - cx, pl.ds(ROW + r - cy, ROW), :])
            scaled = {w: (w * density) * omega for w in sorted(set(WEIGHT))}
            keep = 1.0 - omega
            store(0, x, r, jnp.where(solid, reads[0], keep * reads[0] + scaled[WEIGHT[0]] * still))
            for k in range(1, 19, 2):
                other = OPP[k]
                project = None
                for c in range(3):
                    if CS[k][c]:
                        if project is None:
                            project = u[c] if CS[k][c] > 0 else -u[c]
                        else:
                            project = project + u[c] if CS[k][c] > 0 else project - u[c]
                even = still + 4.5 * project * project
                odd = 3.0 * project
                weight = scaled[WEIGHT[k]]
                store(k, x, r, jnp.where(solid, reads[other], keep * reads[k] + weight * (even + odd)))
                store(other, x, r, jnp.where(solid, reads[k], keep * reads[other] + weight * (even - odd)))

    load_h.wait()
    load_o.wait()
    load_t.wait()
    for x, r in blocks:
        rows = pl.ds(r, ROW)
        code = hl[x, rows, :]
        heat = jnp.zeros((ROW, nz), jnp.float32)
        for level in range(levels):
            heat = jnp.where(code == level, tb[level], heat)
        grid_y = gy * sy + r + row_no
        solid = (
            (ob[x, rows, :] == 1) | (grid_y == 0) | (grid_y == ngy * sy - 1) | first_lane | last_lane
        )
        solid_s[x, rows, :] = jnp.where(solid, 1, 0)
        hb[x + 2, pl.ds(ROW + r, ROW), :] = jnp.where(solid, 0.0, heat)

    load_p.wait()
    own_sums(0, blocks)
    pack_y_raw(0)
    corner_sums(0)
    pl.semaphore_wait(barrier, partners)
    send_corner_raw(0)
    send_corner_sums(0)
    send_x_raw(0)
    send_x_sums(0)
    send_y(0, raw_fields, yr_send, yr_recv)
    send_y(0, sum_fields, ym_send, ym_recv)
    ghost_shares(0)
    await_raw(0)
    finish_peak = spread_all(0, velocity_pass(0, None))
    edge_reads()
    await_sums(0)
    ghost_pass(0, None)

    def store_st1(k, x, r, value):
        st1[k, x, pl.ds(ROW + r, ROW), :] = value

    collided(outer, None, store_st1)
    send_x_raw(1)
    collided(inner, None, store_st1)
    send_corner_raw(1)
    pack_y_raw(1)
    send_y(1, raw_fields, yr_send, yr_recv)
    own_sums(1, outer)
    send_x_sums(1)
    own_sums(1, inner)
    send_y(1, sum_fields, ym_send, ym_recv)
    corner_sums(1)
    send_corner_sums(1)
    send_heat()
    ghost_shares(1)
    await_heat()
    heat_sums()
    fs = finish_peak()
    await_raw(1)
    finish_peak = spread_all(1, velocity_pass(1, fs))
    for x, r in blocks:
        for c in range(3):
            out_v[c, x, pl.ds(r, ROW), :] = vel[c, x + 1, pl.ds(ROW + r, ROW), :]
    edge_reads()
    await_sums(1)
    ghost_pass(1, fs)

    def store_out(k, x, r, value):
        out_p[k, x, pl.ds(r, ROW), :] = value

    collided(blocks, fs, store_out)
    fs = finish_peak()
    lift = {(x, r): fs * hb[x + 2, pl.ds(ROW + r, ROW), :] for x, r in blocks}
    for k in LIFTED:
        for x, r in blocks:
            rows = pl.ds(r, ROW)
            out_p[k, x, rows, :] = out_p[k, x, rows, :] + (3.0 * WEIGHT[k] * CS[k][2]) * lift[(x, r)]
    for sent in gone:
        sent()


def write_out(pops, vel, out_p, out_v, sems):
    copies = [
        pltpu.make_async_copy(pops, out_p, sems.at[0]),
        pltpu.make_async_copy(vel, out_v, sems.at[1]),
    ]
    for copy in copies:
        copy.start()
    for copy in copies:
        copy.wait()


def local(populations, heat_level, obstacle, heat_table):
    ngx = lax.axis_size("gx")
    ngy = lax.axis_size("gy")
    _, sx, sy, nz = populations.shape
    f32 = jnp.float32
    tall = sy + 2 * ROW
    dma = pltpu.SemaphoreType.DMA
    groups = peak_groups(ngx, ngy)
    phases = len(groups)
    vmem = pl.BlockSpec(memory_space=pltpu.VMEM)
    anywhere = pl.BlockSpec(memory_space=pltpu.HBM)
    shapes = (
        jax.ShapeDtypeStruct(populations.shape, f32),
        jax.ShapeDtypeStruct((3, sx, sy, nz), f32),
    )

    def floats(*shape):
        return pltpu.VMEM(shape, f32)

    def ints(*shape):
        return pltpu.VMEM(shape, jnp.int32)

    pops, velocity = pl.pallas_call(
        functools.partial(kernel, ngx, ngy),
        out_shape=shapes,
        in_specs=[anywhere] * 4,
        out_specs=[vmem] * 2,
        scratch_shapes=[
            floats(19, sx, tall, nz),
            floats(19, sx, tall, nz),
            floats(19, sx, sy, nz),
            floats(4, sx, sy, nz),
            floats(sx, sy, nz),
            floats(3, sx + 2, tall, nz),
            ints(sx, sy, nz),
            ints(sx, sy, nz),
            pltpu.SMEM(heat_table.shape, f32),
            ints(sx, sy, nz),
            floats(sx + 4, tall, nz),
            floats(sx + 4, tall, nz),
            floats(sx + 4, tall, nz),
            floats(4, sx + 2, sy, nz),
            floats(4, 2 * sx, nz),
            floats(STEPS, 2, 5, tall, nz),
            floats(STEPS, 2, 4, sy, nz),
            floats(STEPS, 2, 4, sy, nz),
            floats(STEPS, 9, 2 * sx, nz),
            floats(STEPS, 9, 2 * sx, nz),
            floats(8, ROW, nz),
            floats(STEPS, 6, ROW, nz),
            floats(STEPS, ROW, nz),
            floats(STEPS, 6, ROW, nz),
            floats(2, 3, sy, nz),
            floats(4, 2 * sx, nz),
            floats(5, 2 * sx, nz),
            floats(4, 2 * sx, nz),
            floats(2, ROW, nz),
            floats(4, ROW, nz),
            floats(4, 2 * sx, nz),
            floats(2, sy, nz),
            floats(2 * sx, nz),
            floats(STEPS, phases, 1, nz),
            *[floats(STEPS, -(-len(group) // ROW) * ROW, nz) for group in groups],
            dma((4,)),
            *[dma((STEPS, 2))] * 8,
            *[dma((STEPS, 4))] * 4,
            *[dma((8,))] * 2,
            *[dma((STEPS, phases))] * 2,
        ],
        compiler_params=pltpu.CompilerParams(
            collective_id=0, has_side_effects=True, vmem_limit_bytes=24 * 1024 * 1024
        ),
        name="lattice_steps",
    )(*[pltpu.with_memory_space_constraint(a, pltpu.HBM) for a in (populations, heat_level, obstacle, heat_table)])
    return pl.pallas_call(
        write_out,
        out_shape=shapes,
        in_specs=[vmem] * 2,
        out_specs=[anywhere] * 2,
        scratch_shapes=[dma((2,))],
        compiler_params=pltpu.CompilerParams(vmem_limit_bytes=8 * 1024 * 1024),
        name="write_out",
    )(pops, velocity)


def solution(mesh):
    return jax.shard_map(
        local,
        mesh=mesh,
        in_specs=(
            P(None, ("member", "gx"), "gy", None),
            P(("member", "gx"), "gy", None),
            P(("member", "gx"), "gy", None),
            P(),
        ),
        out_specs=(P(None, ("member", "gx"), "gy", None), P(None, ("member", "gx"), "gy", None)),
        check_vma=False,
    )
```

time: 27 us -> 24.9 us (0.922)
  Pallas kernels: 26.2 us -> 24.1 us
    pallas_call x1, Pallas kernels: 25.4 us -> 23.3 us  [local(): pl.pallas_call(functools.partial(kernel, ngx, ngy), out_shape=shapes, in_...]
where the time goes in v1:
time: 24.9 us; the launch traced here: 24.8 us
  Pallas kernels  24.1 us (97%)
  between operations  0.64 us (3%)
    pallas_call x1, Pallas kernels, local(): pl.pallas_call(functools.partial(kernel, ngx, ngy), out_shape=shapes, in_...  23.3 us
    pallas_call x1, Pallas kernels, local(): pl.pallas_call(write_out, out_shape=shapes, in_specs=[vmem] * 2, out_spec...  0.87 us

profile of v1, /device:TPU:0, one launch (start us, length us, event | category | flops | bytes accessed | tf_op | source)
XLA Modules:
  0.0 24.8 jit_solution(15265869223573075386)
XLA Ops:
  0.6 23.3 %lattice_steps.1 = (f32[19,4,16,128]{3,2,1,0:T(8,128)S(1)}, f32[3,4,16,128]{3,2,1,0:T(8,128)S(1)}) custom-call(f32[19,4,16,128]{3,2,1,0:T(8,128)} %pops.1, s32[4,16,128]{2,1,0:T(8,128)} %heat_level.1, s32[4,16,128]{2,1,0:T(8,128)} %obstacle.1, f32[8]{0:T(128)} %table.1), custom_call_target="tpu_custom_call" | custom-call | tf_op jit(solution)/shard_map/lattice_steps/pallas_call | solution.py:705
  23.9 0.9 %write_out.1 = (f32[19,4,16,128]{3,2,1,0:T(8,128)}, f32[3,4,16,128]{3,2,1,0:T(8,128)}) custom-call(f32[19,4,16,128]{3,2,1,0:T(8,128)S(1)} %get-tuple-element.4.pops, f32[3,4,16,128]{3,2,1,0:T(8,128)S(1)} %get-tuple-element.5.vel), custom_call_target="tpu_custom_call" | custom-call | tf_op jit(solution)/shard_map/write_out/pallas_call | solution.py:757

commit v2 on v1

--- a/solution.py
+++ b/solution.py
@@ -69,10 +69,10 @@
     st0, st1, rd, ms, rho_s, vel, hl, ob, tb, solid_s,
     hb, hzp, hzm, hm, hmy,
     xr, xm_out, xm_in, yb_out, yb_in, cg, cm_out, cr_in, cm_in,
-    ox, oy, dr, dm, tu, ex, ey, gfx, gfy, pm_src, *rest,
+    ox, xo_in, oy, dr, dm, tu, ex, ey, gfx, gfy, flat, pm_src, *rest,
 ):
-    (*pm_bufs, load_sem, xr_send, xr_recv, xm_send, xm_recv, yr_send, yr_recv, ym_send, ym_recv,
-     cr_send, cr_recv, cm_send, cm_recv, h_send, h_recv, p_send, p_recv) = rest
+    (*pm_bufs, load_sem, in_sem, x_send, y_send, xr_recv, xm_recv, xo_recv, yr_recv, ym_recv,
+     hx_recv, hy_recv, h2_recv, p_send, p_recv) = rest
     _, sx, sy, nz = pops.shape
     levels = table.shape[0]
     gx = lax.axis_index("gx")
@@ -88,33 +88,36 @@
     y_of = (gy - 1, gy + 1)
     has_y = (has_down, has_up)
 
+    barrier = pltpu.get_barrier_semaphore()
+
+    def greet(sem, x, y):
+        pl.semaphore_signal(sem, inc=1, device_id={"gx": x, "gy": y}, device_id_type=pl.DeviceIdType.MESH)
+
+    groups = peak_groups(ngx, ngy)
+    beside = sorted({1, ngx - 1} - {0})
+    column = [(0, dy) for dy in range(1, ngy)]
+    by_word = len(groups) == 1 and ngx <= 5
+    greeted = [(dx, 0) for dx in beside] + column if by_word else [place for group in groups for place in group]
+    partners = len(greeted)
+    for dx, dy in greeted:
+        greet(barrier, lax.rem(gx + dx, ngx), lax.rem(gy + dy, ngy))
+    if len(groups) > 1:
+        partners = partners + 2 * (jnp.where(has_up, 1, 0) + jnp.where(has_down, 1, 0))
+        for s in (0, 1):
+
+            @pl.when(has_y[s])
+            def _():
+                greet(barrier, right, y_of[s])
+                greet(barrier, left, y_of[s])
+
     load_p = pltpu.make_async_copy(pops, st0.at[:, :, own_y, :], load_sem.at[0])
     load_h = pltpu.make_async_copy(heat_level, hl, load_sem.at[1])
     load_o = pltpu.make_async_copy(obstacle, ob, load_sem.at[2])
+    load_t = pltpu.make_async_copy(table, tb, load_sem.at[3])
     load_p.start()
     load_h.start()
     load_o.start()
-    load_t = pltpu.make_async_copy(table, tb, load_sem.at[3])
     load_t.start()
-
-    barrier = pltpu.get_barrier_semaphore()
-
-    def greet(x, y):
-        pl.semaphore_signal(barrier, inc=1, device_id={"gx": x, "gy": y}, device_id_type=pl.DeviceIdType.MESH)
-
-    groups = peak_groups(ngx, ngy)
-    partners = sum(len(group) for group in groups)
-    for group in groups:
-        for dx, dy in group:
-            greet(lax.rem(gx + dx, ngx), lax.rem(gy + dy, ngy))
-    if len(groups) > 1:
-        partners = partners + 2 * (jnp.where(has_up, 1, 0) + jnp.where(has_down, 1, 0))
-        for s in (0, 1):
-
-            @pl.when(has_y[s])
-            def _():
-                greet(right, y_of[s])
-                greet(left, y_of[s])
 
     def zeros(ref, *index):
         part = ref.at[index]
@@ -140,8 +143,6 @@
                 zeros(cm_in, every, every, pl.ds(xs * 2 + s, 1), every)
             zeros(hb, every, pl.ds((ROW - 2, ROW + sy)[s], 2), every)
 
-    gone = []
-
     def guarded(cond, fn):
         if cond is None:
             fn()
@@ -161,18 +162,14 @@
     def await_bytes(cond, view, sem):
         guarded(cond, lambda: pltpu.make_async_copy(view, view, sem).wait())
 
-    def send_later(cond, view, sem):
-        gone.append(lambda: await_bytes(cond, view, sem))
-
     states = (st0, st1)
-
-    def x_raw(step, s):
-        st = states[step]
-        return [(st.at[k, face_x[s], own_y, :], xr.at[step, 1 - s, j, own_y, :]) for j, k in enumerate(ACROSS_X[OUT[s]])]
-
-    def send_x_raw(step):
+    corners = [(xs, ys) for xs in (0, 1) for ys in (0, 1)]
+    raw_fields = pl.ds(0, 5)
+    sum_fields = pl.ds(5, 4)
+
+    def along_x(pairs_of, recv_sem):
         def go(s):
-            send(None, x_raw(step, s), xr_send.at[step, s], xr_recv.at[step, 1 - s], x_of[s], gy)
+            send(None, pairs_of(s), x_send, recv_sem, x_of[s], gy)
 
         @pl.when(gx == 0)
         def _():
@@ -184,96 +181,98 @@
             go(1)
             go(0)
 
-        for s in (0, 1):
-            send_later(None, states[step].at[pl.ds(0, 5), 0, own_y, :], xr_send.at[step, s])
+    def send_x_raw(step):
+        st = states[step]
+        along_x(
+            lambda s: [(st.at[k, face_x[s], own_y, :], xr.at[step, 1 - s, j, own_y, :]) for j, k in enumerate(ACROSS_X[OUT[s]])],
+            xr_recv.at[step],
+        )
 
     def send_x_sums(step):
-        def go(s):
-            send(None, [(xm_out.at[step, s], xm_in.at[step, 1 - s])], xm_send.at[step, s], xm_recv.at[step, 1 - s], x_of[s], gy)
-
-        @pl.when(gx == 0)
-        def _():
-            go(0)
-            go(1)
-
-        @pl.when(gx != 0)
-        def _():
-            go(1)
-            go(0)
-
-        for s in (0, 1):
-            send_later(None, xm_out.at[step, s], xm_send.at[step, s])
-
-    def send_y(step, fields, send_sem, recv_sem):
+        along_x(lambda s: [(xm_out.at[step, s], xm_in.at[step, 1 - s])], xm_recv.at[step])
+
+    def send_x_shares():
+        along_x(lambda s: [(ox.at[s], xo_in.at[1 - s])], xo_recv)
+
+    def send_heat_x(recv_sem, near):
+        at = ((2, sx + 1), (sx + 2, 1)) if near else ((3, sx), (sx + 3, 0))
+        along_x(lambda s: [(hb.at[at[0][s], own_y, :], hb.at[at[1][s], own_y, :])], recv_sem)
+
+    def send_y(step, fields, recv_sem):
         for s in (0, 1):
             src = yb_out.at[step, fields, pl.ds(s * sx, sx), :]
             dst = yb_in.at[step, fields, pl.ds((1 - s) * sx, sx), :]
-            send(has_y[s], [(src, dst)], send_sem.at[step, s], recv_sem.at[step, 1 - s], gx, y_of[s])
-            send_later(has_y[s], src, send_sem.at[step, s])
-
-    corners = [(xs, ys) for xs in (0, 1) for ys in (0, 1)]
+            send(has_y[s], [(src, dst)], y_send.at[s], recv_sem.at[step, 1 - s], gx, y_of[s])
+
+    def send_heat_y():
+        for s in (0, 1):
+            src = hb.at[pl.ds(2, sx), pl.ds((ROW, ROW + sy - 2)[s], 2), :]
+            dst = hb.at[pl.ds(2, sx), pl.ds((ROW + sy, ROW - 2)[s], 2), :]
+            send(has_y[s], [(src, dst)], y_send.at[s], hy_recv.at[1 - s], gx, y_of[s])
+
+    def to_corners(pair_of, sem_of):
+        for c, (xs, ys) in enumerate(corners):
+            send(has_y[ys], [pair_of(c, xs, ys)], y_send.at[ys], sem_of(1 - ys), x_of[xs], y_of[ys])
 
     def send_corner_raw(step):
         st = states[step]
-        for c, (xs, ys) in enumerate(corners):
+
+        def pair(c, xs, ys):
             k = NUMBER[(OUT[xs], OUT[ys], 0)]
-            src = st.at[k, face_x[xs], pl.ds(ROW + edge_y[ys], 1), :]
-            send(has_y[ys], [(src, cr_in.at[step, pl.ds(3 - c, 1), :])], cr_send.at[step, c], cr_recv.at[step, 3 - c], x_of[xs], y_of[ys])
-            send_later(has_y[ys], src, cr_send.at[step, c])
+            return st.at[k, face_x[xs], pl.ds(ROW + edge_y[ys], 1), :], cr_in.at[step, pl.ds(3 - c, 1), :]
+
+        to_corners(pair, lambda s: yr_recv.at[step, s])
 
     def send_corner_sums(step):
-        for c, (xs, ys) in enumerate(corners):
-            src = cm_out.at[step, :, pl.ds(c, 1), :]
-            send(has_y[ys], [(src, cm_in.at[step, :, pl.ds(3 - c, 1), :])], cm_send.at[step, c], cm_recv.at[step, 3 - c], x_of[xs], y_of[ys])
-            send_later(has_y[ys], src, cm_send.at[step, c])
-
-    def await_raw(step):
-        for s in (0, 1):
-            await_bytes(has_y[s], yb_in.at[step, pl.ds(0, 5), pl.ds(s * sx, sx), :], yr_recv.at[step, s])
-        for c, (xs, ys) in enumerate(corners):
-            await_bytes(has_y[ys], cr_in.at[step, pl.ds(c, 1), :], cr_recv.at[step, c])
-        for s in (0, 1):
-            await_bytes(None, xr.at[step, s, :, own_y, :], xr_recv.at[step, s])
+        to_corners(
+            lambda c, xs, ys: (cm_out.at[step, :, pl.ds(c, 1), :], cm_in.at[step, :, pl.ds(3 - c, 1), :]),
+            lambda s: ym_recv.at[step, s],
+        )
+
+    def send_heat_corner():
+        to_corners(
+            lambda c, xs, ys: (
+                hb.at[2 + face_x[xs], pl.ds(ROW + edge_y[ys], 1), :],
+                hb.at[(sx + 2, 1)[xs], pl.ds((ROW + sy, ROW - 1)[ys], 1), :],
+            ),
+            lambda s: h2_recv.at[s],
+        )
+
+    def await_y_raw(step):
+        for s in (0, 1):
+            await_bytes(has_y[s], flat.at[pl.ds(0, 5 * sx + 2), :], yr_recv.at[step, s])
+
+    def await_x_raw(step):
+        await_bytes(None, xr.at[step, :, :, own_y, :], xr_recv.at[step])
 
     def await_sums(step):
         for s in (0, 1):
-            await_bytes(has_y[s], yb_in.at[step, pl.ds(5, 4), pl.ds(s * sx, sx), :], ym_recv.at[step, s])
-        for c, (xs, ys) in enumerate(corners):
-            await_bytes(has_y[ys], cm_in.at[step, :, pl.ds(c, 1), :], cm_recv.at[step, c])
-        for s in (0, 1):
-            await_bytes(None, xm_in.at[step, s], xm_recv.at[step, s])
-
-    raw_fields = pl.ds(0, 5)
-    sum_fields = pl.ds(5, 4)
-
-    def heat_moves():
-        moves = []
-        layers = ((2, sx), (0, sx + 2))
-        for s in (0, 1):
-            src = hb.at[pl.ds(layers[0][s], 2), own_y, :]
-            dst = hb.at[pl.ds((sx + 2, 0)[s], 2), own_y, :]
-            moves.append((None, src, dst, x_of[s], gy))
-        for s in (0, 1):
-            src = hb.at[pl.ds(2, sx), pl.ds((ROW, ROW + sy - 2)[s], 2), :]
-            dst = hb.at[pl.ds(2, sx), pl.ds((ROW + sy, ROW - 2)[s], 2), :]
-            moves.append((has_y[s], src, dst, gx, y_of[s]))
-        for xs, ys in corners:
-            src = hb.at[2 + face_x[xs], pl.ds(ROW + edge_y[ys], 1), :]
-            dst = hb.at[(sx + 2, 1)[xs], pl.ds((ROW + sy, ROW - 1)[ys], 1), :]
-            moves.append((has_y[ys], src, dst, x_of[xs], y_of[ys]))
-        return moves
-
-    arrives_on = (1, 0, 3, 2, 7, 6, 5, 4)
-
-    def send_heat():
-        for number, (cond, src, dst, x, y) in enumerate(heat_moves()):
-            send(cond, [(src, dst)], h_send.at[number], h_recv.at[number], x, y)
-            send_later(cond, src, h_send.at[number])
-
-    def await_heat():
-        moves = heat_moves()
-        for number, (_, src, dst, _, _) in enumerate(moves):
-            await_bytes(moves[arrives_on[number]][0], dst, h_recv.at[number])
+            await_bytes(has_y[s], flat.at[pl.ds(0, 4 * sx + 12), :], ym_recv.at[step, s])
+        await_bytes(None, xm_in.at[step], xm_recv.at[step])
+
+    def await_near_heat():
+        for s in (0, 1):
+            await_bytes(has_y[s], hb.at[pl.ds(2, sx), pl.ds(ROW, 2), :], hy_recv.at[s])
+        await_bytes(None, hb.at[pl.ds(0, 2), own_y, :], hx_recv.at[0])
+
+    def await_far_heat():
+        for s in (0, 1):
+            await_bytes(has_y[s], flat.at[pl.ds(0, 2), :], h2_recv.at[s])
+        await_bytes(None, hb.at[pl.ds(0, 2), own_y, :], hx_recv.at[1])
+
+    def await_sends():
+        for view in (xr.at[:, :, :, own_y, :], xm_out, ox, hb.at[pl.ds(0, 4), own_y, :]):
+            await_bytes(None, view, x_send)
+        for s in (0, 1):
+            for view in (
+                yb_out.at[:, :, pl.ds(0, sx), :],
+                hb.at[pl.ds(2, sx), pl.ds(ROW, 2), :],
+                flat.at[pl.ds(0, STEPS * 14 + 2), :],
+            ):
+                await_bytes(has_y[s], view, y_send.at[s])
+        for phase, group in enumerate(groups):
+            for step in range(STEPS):
+                await_bytes(None, pm_bufs[phase].at[step, pl.ds(0, len(group)), :], p_send.at[phase])
 
     def spread(step, phase, value):
         group = peak_groups(ngx, ngy)[phase]
@@ -285,13 +284,12 @@
             pltpu.make_async_remote_copy(
                 src_ref=pm_src.at[step, phase],
                 dst_ref=buf.at[step, pl.ds(d - 1, 1), :],
-                send_sem=p_send.at[step, phase],
+                send_sem=p_send.at[phase],
                 recv_sem=p_recv.at[step, phase],
                 device_id=place,
                 device_id_type=pl.DeviceIdType.MESH,
             ).start()
         view = buf.at[step, pl.ds(0, count), :]
-        send_later(None, view, p_send.at[step, phase])
 
         def wait():
             await_bytes(None, view, p_recv.at[step, phase])
@@ -396,7 +394,7 @@
                 minus = jnp.where(pack_row == ys * sx + sx - 1, fill(2 + ys), minus)
         return [fields[0], plus, minus, shift_z(fields[3], 1), shift_z(fields[4], -1)]
 
-    def ghost_shares(step):
+    def face_shares(step):
         st = states[step]
         for s in (0, 1):
             for r in range(0, sy, ROW):
@@ -406,6 +404,8 @@
                 ox[s, 0, pl.ds(r, ROW), :] = ((a + b) + (c + d)) + e
                 ox[s, 1, pl.ds(r, ROW), :] = b - c
                 ox[s, 2, pl.ds(r, ROW), :] = d - e
+
+    def edge_shares(step):
         a, b, c, d, e = packed([yb_out[step, j] for j in range(5)], None)
         total = ((a + b) + (c + d)) + e
         oy[0] = total
@@ -427,17 +427,15 @@
             sums = [ms[m, x, rows, :] for m in range(4)]
             for s in (0, 1):
                 if x == face_x[s]:
-                    ks = ACROSS_X[IN[s]]
-                    parts = [
-                        shift_z(xr[step, s, j, pl.ds(ROW + r - CS[k][1], ROW), :], CS[k][2]) for j, k in enumerate(ks)
-                    ]
-                    for k, part in zip(ks, parts):
-                        rd[k, x, rows, :] = part
-                    share = tree_sum(parts)
-                    sums[0] = sums[0] + share
-                    sums[1] = sums[1] + share if s == 0 else sums[1] - share
-                    sums[2] = sums[2] + (parts[1] - parts[2])
-                    sums[3] = sums[3] + (parts[3] - parts[4])
+                    if step == 0:
+                        parts = face_reads(step, s, r)
+                        shares = tree_sum(parts), parts[1] - parts[2], parts[3] - parts[4]
+                    else:
+                        shares = [xo_in[s, m, rows, :] for m in range(3)]
+                    sums[0] = sums[0] + shares[0]
+                    sums[1] = sums[1] + shares[0] if s == 0 else sums[1] - shares[0]
+                    sums[2] = sums[2] + shares[1]
+                    sums[3] = sums[3] + shares[2]
             for s in edges_of(r):
                 for m in range(4):
                     sums[m] = sums[m] + jnp.where(edge_row[s], dm[m, pl.ds(s * sx + x, 1), :], 0.0)
@@ -453,6 +451,14 @@
                 speed.append(u * u)
             peak = jnp.maximum(peak, speed[0] + speed[1] + speed[2])
         return peak
+
+    def face_reads(step, s, r):
+        parts = []
+        for j, k in enumerate(ACROSS_X[IN[s]]):
+            part = shift_z(xr[step, s, j, pl.ds(ROW + r - CS[k][1], ROW), :], CS[k][2])
+            rd[k, face_x[s], pl.ds(r, ROW), :] = part
+            parts.append(part)
+        return parts
 
     def edge_reads():
         for s in (0, 1):
@@ -510,40 +516,52 @@
                     at = s * sx + x
                     vel[c, x + 1, pl.ds((ROW - 1, ROW + sy)[s], 1), :] = u[at : at + 1, :]
 
-    def heat_sums():
-        for x in range(sx + 4):
-            spans = [(ROW + r, ROW) for r in range(0, sy, ROW)]
-            if 1 <= x <= sx + 2:
-                spans += [(ROW - 2, 2), (ROW + sy, 2)]
-            for at, span in spans:
-                if span != ROW and x in (1, sx + 2):
-                    at, span = (at + 1, 1) if at < ROW else (at, 1)
-                cells = hb[x, pl.ds(at, span), :]
-                hzp[x, pl.ds(at, span), :] = shift_z(cells, 1)
-                hzm[x, pl.ds(at, span), :] = shift_z(cells, -1)
-
-        def at(x, row, span):
-            cells = [
-                (hzp[i, pl.ds(y, span), :], hzm[i, pl.ds(y, span), :])
-                for i, y in ((x, row), (x - 1, row), (x + 1, row), (x, row - 1), (x, row + 1))
-            ]
-            diff = [a - b for a, b in cells]
-            both = [a + b for a, b in cells]
-            main, side = 3.0 * WEIGHT[5], 3.0 * WEIGHT[11]
-            return (
-                main * diff[0] + side * ((diff[1] + diff[2]) + (diff[3] + diff[4])),
-                side * (diff[1] - diff[2]),
-                side * (diff[3] - diff[4]),
-                main * both[0] + side * ((both[1] + both[2]) + (both[3] + both[4])),
-            )
-
-        for x in range(sx + 2):
+    def shift_heat(x, row, span):
+        cells = hb[x, pl.ds(row, span), :]
+        hzp[x, pl.ds(row, span), :] = shift_z(cells, 1)
+        hzm[x, pl.ds(row, span), :] = shift_z(cells, -1)
+
+    def heat_moments(x, row, span):
+        cells = [
+            (hzp[i, pl.ds(y, span), :], hzm[i, pl.ds(y, span), :])
+            for i, y in ((x, row), (x - 1, row), (x + 1, row), (x, row - 1), (x, row + 1))
+        ]
+        diff = [a - b for a, b in cells]
+        both = [a + b for a, b in cells]
+        main, side = 3.0 * WEIGHT[5], 3.0 * WEIGHT[11]
+        return (
+            main * diff[0] + side * ((diff[1] + diff[2]) + (diff[3] + diff[4])),
+            side * (diff[1] - diff[2]),
+            side * (diff[3] - diff[4]),
+            main * both[0] + side * ((both[1] + both[2]) + (both[3] + both[4])),
+        )
+
+    def heat_sums(columns):
+        for x in columns:
             for r in range(0, sy, ROW):
-                for m, value in enumerate(at(x + 1, ROW + r, ROW)):
+                for m, value in enumerate(heat_moments(x + 1, ROW + r, ROW)):
                     hm[m, x, pl.ds(r, ROW), :] = value
+
+    def near_heat():
+        for x in range(1, sx + 3):
+            for r in range(0, sy, ROW):
+                shift_heat(x, ROW + r, ROW)
+        for x in range(2, sx + 2):
+            shift_heat(x, ROW - 2, 2)
+            shift_heat(x, ROW + sy, 2)
+        heat_sums(range(1, sx + 1))
+
+    def far_heat():
+        for x in (0, sx + 3):
+            for r in range(0, sy, ROW):
+                shift_heat(x, ROW + r, ROW)
+        for x in (1, sx + 2):
+            shift_heat(x, ROW - 1, 1)
+            shift_heat(x, ROW + sy, 1)
+        heat_sums((0, sx + 1))
         for s in (0, 1):
             for x in range(sx):
-                for m, value in enumerate(at(x + 2, (ROW - 1, ROW + sy)[s], 1)):
+                for m, value in enumerate(heat_moments(x + 2, (ROW - 1, ROW + sy)[s], 1)):
                     hmy[m, pl.ds(s * sx + x, 1), :] = value
 
     def collided(tiles, fs, store):
@@ -611,46 +629,67 @@
     load_p.wait()
     own_sums(0, blocks)
     pack_y_raw(0)
-    corner_sums(0)
+    if not by_word:
+        corner_sums(0)
     pl.semaphore_wait(barrier, partners)
+    if by_word:
+        for dx, dy in column:
+            greet(in_sem, gx, lax.rem(gy + dy, ngy))
+    send_x_raw(0)
+    send_x_sums(0)
+    send_y(0, raw_fields, yr_recv)
+    send_y(0, sum_fields, ym_recv)
+    if by_word:
+        corner_sums(0)
+        pl.semaphore_wait(in_sem, len(column))
     send_corner_raw(0)
     send_corner_sums(0)
-    send_x_raw(0)
-    send_x_sums(0)
-    send_y(0, raw_fields, yr_send, yr_recv)
-    send_y(0, sum_fields, ym_send, ym_recv)
-    ghost_shares(0)
-    await_raw(0)
+    face_shares(0)
+    edge_shares(0)
+    await_y_raw(0)
+    await_x_raw(0)
+    await_sums(0)
     finish_peak = spread_all(0, velocity_pass(0, None))
+    send_heat_x(hx_recv.at[0], True)
+    send_heat_y()
     edge_reads()
-    await_sums(0)
     ghost_pass(0, None)
 
     def store_st1(k, x, r, value):
         st1[k, x, pl.ds(ROW + r, ROW), :] = value
 
     collided(outer, None, store_st1)
-    send_x_raw(1)
+    face_shares(1)
+    send_x_shares()
     collided(inner, None, store_st1)
     send_corner_raw(1)
     pack_y_raw(1)
-    send_y(1, raw_fields, yr_send, yr_recv)
+    send_y(1, raw_fields, yr_recv)
+    send_x_raw(1)
     own_sums(1, outer)
     send_x_sums(1)
     own_sums(1, inner)
-    send_y(1, sum_fields, ym_send, ym_recv)
+    send_y(1, sum_fields, ym_recv)
     corner_sums(1)
     send_corner_sums(1)
-    send_heat()
-    ghost_shares(1)
-    await_heat()
-    heat_sums()
+    send_heat_x(hx_recv.at[1], False)
+    send_heat_corner()
+    edge_shares(1)
+    await_near_heat()
+    near_heat()
     fs = finish_peak()
-    await_raw(1)
+    await_y_raw(1)
+    await_bytes(None, xo_in, xo_recv)
     finish_peak = spread_all(1, velocity_pass(1, fs))
     for x, r in blocks:
         for c in range(3):
             out_v[c, x, pl.ds(r, ROW), :] = vel[c, x + 1, pl.ds(ROW + r, ROW), :]
+    await_far_heat()
+    far_heat()
+    await_x_raw(1)
+    for s in (0, 1):
+        for r in range(0, sy, ROW):
+            face_reads(1, s, r)
     edge_reads()
     await_sums(1)
     ghost_pass(1, fs)
@@ -659,14 +698,13 @@
         out_p[k, x, pl.ds(r, ROW), :] = value
 
     collided(blocks, fs, store_out)
+    await_sends()
     fs = finish_peak()
     lift = {(x, r): fs * hb[x + 2, pl.ds(ROW + r, ROW), :] for x, r in blocks}
     for k in LIFTED:
         for x, r in blocks:
             rows = pl.ds(r, ROW)
             out_p[k, x, rows, :] = out_p[k, x, rows, :] + (3.0 * WEIGHT[k] * CS[k][2]) * lift[(x, r)]
-    for sent in gone:
-        sent()
 
 
 def write_out(pops, vel, out_p, out_v, sems):
@@ -733,6 +771,7 @@
             floats(STEPS, ROW, nz),
             floats(STEPS, 6, ROW, nz),
             floats(2, 3, sy, nz),
+            floats(2, 3, sy, nz),
             floats(4, 2 * sx, nz),
             floats(5, 2 * sx, nz),
             floats(4, 2 * sx, nz),
@@ -741,13 +780,23 @@
             floats(4, 2 * sx, nz),
             floats(2, sy, nz),
             floats(2 * sx, nz),
+            floats(8 * ROW, nz),
             floats(STEPS, phases, 1, nz),
             *[floats(STEPS, -(-len(group) // ROW) * ROW, nz) for group in groups],
             dma((4,)),
-            *[dma((STEPS, 2))] * 8,
-            *[dma((STEPS, 4))] * 4,
-            *[dma((8,))] * 2,
-            *[dma((STEPS, phases))] * 2,
+            pltpu.SemaphoreType.REGULAR,
+            dma,
+            dma((2,)),
+            dma((STEPS,)),
+            dma((STEPS,)),
+            dma,
+            dma((STEPS, 2)),
+            dma((STEPS, 2)),
+            dma((2,)),
+            dma((2,)),
+            dma((2,)),
+            dma((phases,)),
+            dma((STEPS, phases)),
         ],
         compiler_params=pltpu.CompilerParams(
             collective_id=0, has_side_effects=True, vmem_limit_bytes=24 * 1024 * 1024

time: 24.9 us -> 22.2 us (0.89)
  Pallas kernels: 24.1 us -> 21.4 us
    pallas_call x1, Pallas kernels: 23.3 us -> 20.5 us  [local(): pl.pallas_call(functools.partial(kernel, ngx, ngy), out_shape=shapes, in_...]
where the time goes in v2:
time: 22.2 us; the launch traced here: 22 us
  Pallas kernels  21.4 us (96%)
  between operations  0.64 us (3%)
    pallas_call x1, Pallas kernels, local(): pl.pallas_call(functools.partial(kernel, ngx, ngy), out_shape=shapes, in_...  20.5 us
    pallas_call x1, Pallas kernels, local(): pl.pallas_call(write_out, out_shape=shapes, in_specs=[vmem] * 2, out_spec...  0.87 us

profile of v2, /device:TPU:0, one launch (start us, length us, event | category | flops | bytes accessed | tf_op | source)
XLA Modules:
  0.0 22.0 jit_solution(1917450829753671471)
XLA Ops:
  0.6 20.5 %lattice_steps.1 = (f32[19,4,16,128]{3,2,1,0:T(8,128)S(1)}, f32[3,4,16,128]{3,2,1,0:T(8,128)S(1)}) custom-call(f32[19,4,16,128]{3,2,1,0:T(8,128)} %pops.1, s32[4,16,128]{2,1,0:T(8,128)} %heat_level.1, s32[4,16,128]{2,1,0:T(8,128)} %obstacle.1, f32[8]{0:T(128)} %table.1), custom_call_target="tpu_custom_call" | custom-call | tf_op jit(solution)/shard_map/lattice_steps/pallas_call | solution.py:743
  21.2 0.9 %write_out.1 = (f32[19,4,16,128]{3,2,1,0:T(8,128)}, f32[3,4,16,128]{3,2,1,0:T(8,128)}) custom-call(f32[19,4,16,128]{3,2,1,0:T(8,128)S(1)} %get-tuple-element.4.pops, f32[3,4,16,128]{3,2,1,0:T(8,128)S(1)} %get-tuple-element.5.vel), custom_call_target="tpu_custom_call" | custom-call | tf_op jit(solution)/shard_map/write_out/pallas_call | solution.py:806

commit v3 on v2

--- a/solution.py
+++ b/solution.py
@@ -69,10 +69,10 @@
     st0, st1, rd, ms, rho_s, vel, hl, ob, tb, solid_s,
     hb, hzp, hzm, hm, hmy,
     xr, xm_out, xm_in, yb_out, yb_in, cg, cm_out, cr_in, cm_in,
-    ox, xo_in, oy, dr, dm, tu, ex, ey, gfx, gfy, flat, pm_src, *rest,
+    ox, ox2, xo_in, x2_in, oy, dr, dm, tu, ex, ey, gfx, gfy, flat, pm_src, *rest,
 ):
-    (*pm_bufs, load_sem, in_sem, x_send, y_send, xr_recv, xm_recv, xo_recv, yr_recv, ym_recv,
-     hx_recv, hy_recv, h2_recv, p_send, p_recv) = rest
+    (*pm_bufs, load_sem, in_sem, col_sem, x_send, y_send, xr_recv, xm_recv, xo_recv, yr_recv, ym_recv,
+     hx_recv, hy_recv, p_send, p_recv) = rest
     _, sx, sy, nz = pops.shape
     levels = table.shape[0]
     gx = lax.axis_index("gx")
@@ -129,7 +129,7 @@
             for c in (1, -1):
                 for k in ACROSS_Y[c]:
                     zeros(st, k, every, pl.ds(row, 1), every)
-        zeros(xr, every, every, every, pl.ds(row, 1), every)
+        zeros(xr, every, every, pl.ds(row, 1), every)
     for ref in (cg, tu, ey):
         ref[...] = jnp.zeros(ref.shape, jnp.float32)
 
@@ -167,48 +167,56 @@
     raw_fields = pl.ds(0, 5)
     sum_fields = pl.ds(5, 4)
 
+    at_end = (gx == 0, gx == ngx - 1)
+
     def along_x(pairs_of, recv_sem):
-        def go(s):
-            send(None, pairs_of(s), x_send, recv_sem, x_of[s], gy)
-
-        @pl.when(gx == 0)
-        def _():
-            go(0)
-            go(1)
-
-        @pl.when(gx != 0)
-        def _():
-            go(1)
-            go(0)
-
-    def send_x_raw(step):
-        st = states[step]
-        along_x(
-            lambda s: [(st.at[k, face_x[s], own_y, :], xr.at[step, 1 - s, j, own_y, :]) for j, k in enumerate(ACROSS_X[OUT[s]])],
-            xr_recv.at[step],
+        def far():
+            for s in (0, 1):
+                send(at_end[s], pairs_of(s), x_send, recv_sem, x_of[s], gy)
+
+        def near():
+            for s in (0, 1):
+                send(jnp.logical_not(at_end[s]), pairs_of(s), x_send, recv_sem, x_of[s], gy)
+
+        return far, near
+
+    def send_x_raw():
+        return along_x(
+            lambda s: [(st0.at[k, face_x[s], own_y, :], xr.at[1 - s, j, own_y, :]) for j, k in enumerate(ACROSS_X[OUT[s]])],
+            xr_recv.at[0],
         )
 
     def send_x_sums(step):
-        along_x(lambda s: [(xm_out.at[step, s], xm_in.at[step, 1 - s])], xm_recv.at[step])
+        return along_x(lambda s: [(xm_out.at[step, s], xm_in.at[step, 1 - s])], xm_recv.at[step])
+
+    rest_rows = pl.ds(0, 2 * sy + 2)
 
     def send_x_shares():
-        along_x(lambda s: [(ox.at[s], xo_in.at[1 - s])], xo_recv)
-
-    def send_heat_x(recv_sem, near):
-        at = ((2, sx + 1), (sx + 2, 1)) if near else ((3, sx), (sx + 3, 0))
-        along_x(lambda s: [(hb.at[at[0][s], own_y, :], hb.at[at[1][s], own_y, :])], recv_sem)
+        return along_x(lambda s: [(ox.at[s], xo_in.at[1 - s])], xo_recv)
+
+    def send_x_rest():
+        return along_x(lambda s: [(ox2.at[s, rest_rows, :], x2_in.at[1 - s, rest_rows, :])], xr_recv.at[1])
+
+    def send_heat():
+        for part in along_x(lambda s: [(hb.at[pl.ds((2, sx)[s], 2), own_y, :], hb.at[pl.ds((sx + 2, 0)[s], 2), own_y, :])], hx_recv):
+            part()
+        for s in (0, 1):
+            src = hb.at[pl.ds(2, sx), pl.ds((ROW, ROW + sy - 2)[s], 2), :]
+            dst = hb.at[pl.ds(2, sx), pl.ds((ROW + sy, ROW - 2)[s], 2), :]
+            send(has_y[s], [(src, dst)], y_send.at[s], hy_recv.at[1 - s], gx, y_of[s])
+        to_corners(
+            lambda c, xs, ys: (
+                hb.at[2 + face_x[xs], pl.ds(ROW + edge_y[ys], 1), :],
+                hb.at[(sx + 2, 1)[xs], pl.ds((ROW + sy, ROW - 1)[ys], 1), :],
+            ),
+            lambda s: hy_recv.at[s],
+        )
 
     def send_y(step, fields, recv_sem):
         for s in (0, 1):
             src = yb_out.at[step, fields, pl.ds(s * sx, sx), :]
             dst = yb_in.at[step, fields, pl.ds((1 - s) * sx, sx), :]
             send(has_y[s], [(src, dst)], y_send.at[s], recv_sem.at[step, 1 - s], gx, y_of[s])
-
-    def send_heat_y():
-        for s in (0, 1):
-            src = hb.at[pl.ds(2, sx), pl.ds((ROW, ROW + sy - 2)[s], 2), :]
-            dst = hb.at[pl.ds(2, sx), pl.ds((ROW + sy, ROW - 2)[s], 2), :]
-            send(has_y[s], [(src, dst)], y_send.at[s], hy_recv.at[1 - s], gx, y_of[s])
 
     def to_corners(pair_of, sem_of):
         for c, (xs, ys) in enumerate(corners):
@@ -229,46 +237,31 @@
             lambda s: ym_recv.at[step, s],
         )
 
-    def send_heat_corner():
-        to_corners(
-            lambda c, xs, ys: (
-                hb.at[2 + face_x[xs], pl.ds(ROW + edge_y[ys], 1), :],
-                hb.at[(sx + 2, 1)[xs], pl.ds((ROW + sy, ROW - 1)[ys], 1), :],
-            ),
-            lambda s: h2_recv.at[s],
-        )
-
     def await_y_raw(step):
         for s in (0, 1):
             await_bytes(has_y[s], flat.at[pl.ds(0, 5 * sx + 2), :], yr_recv.at[step, s])
 
-    def await_x_raw(step):
-        await_bytes(None, xr.at[step, :, :, own_y, :], xr_recv.at[step])
+    def await_x_raw():
+        await_bytes(None, xr.at[:, :, own_y, :], xr_recv.at[0])
+
+    def await_x_rest():
+        await_bytes(None, x2_in.at[:, rest_rows, :], xr_recv.at[1])
 
     def await_sums(step):
         for s in (0, 1):
             await_bytes(has_y[s], flat.at[pl.ds(0, 4 * sx + 12), :], ym_recv.at[step, s])
         await_bytes(None, xm_in.at[step], xm_recv.at[step])
 
-    def await_near_heat():
-        for s in (0, 1):
-            await_bytes(has_y[s], hb.at[pl.ds(2, sx), pl.ds(ROW, 2), :], hy_recv.at[s])
-        await_bytes(None, hb.at[pl.ds(0, 2), own_y, :], hx_recv.at[0])
-
-    def await_far_heat():
-        for s in (0, 1):
-            await_bytes(has_y[s], flat.at[pl.ds(0, 2), :], h2_recv.at[s])
-        await_bytes(None, hb.at[pl.ds(0, 2), own_y, :], hx_recv.at[1])
+    def await_heat():
+        for s in (0, 1):
+            await_bytes(has_y[s], flat.at[pl.ds(0, 2 * sx + 2), :], hy_recv.at[s])
+        await_bytes(None, hb.at[pl.ds(0, 4), own_y, :], hx_recv)
 
     def await_sends():
-        for view in (xr.at[:, :, :, own_y, :], xm_out, ox, hb.at[pl.ds(0, 4), own_y, :]):
+        for view in (xr.at[:, :, own_y, :], xm_out, ox, ox2.at[:, rest_rows, :], hb.at[pl.ds(0, 4), own_y, :]):
             await_bytes(None, view, x_send)
         for s in (0, 1):
-            for view in (
-                yb_out.at[:, :, pl.ds(0, sx), :],
-                hb.at[pl.ds(2, sx), pl.ds(ROW, 2), :],
-                flat.at[pl.ds(0, STEPS * 14 + 2), :],
-            ):
+            for view in (yb_out.at[:, :, pl.ds(0, sx), :], flat.at[pl.ds(0, 2 * sx + STEPS * 14 + 2), :]):
                 await_bytes(has_y[s], view, y_send.at[s])
         for phase, group in enumerate(groups):
             for step in range(STEPS):
@@ -305,7 +298,7 @@
             for phase in range(1, len(pm_bufs)):
                 best = spread(step, phase, best)()
             peak = jnp.broadcast_to(jnp.max(best, axis=1, keepdims=True), (ROW, nz))
-            return speed_cap / jnp.sqrt(speed_cap * speed_cap + peak)
+            return speed_cap * lax.rsqrt(speed_cap * speed_cap + peak)
 
         return finish
 
@@ -404,6 +397,12 @@
                 ox[s, 0, pl.ds(r, ROW), :] = ((a + b) + (c + d)) + e
                 ox[s, 1, pl.ds(r, ROW), :] = b - c
                 ox[s, 2, pl.ds(r, ROW), :] = d - e
+                if step == 1:
+                    ox2[s, pl.ds(r, ROW), :] = b
+                    ox2[s, pl.ds(sy + r, ROW), :] = d
+            if step == 1:
+                ox2[s, pl.ds(2 * sy, 1), :] = st[ACROSS_X[OUT[s]][2], face_x[s], pl.ds(ROW, 1), :]
+                ox2[s, pl.ds(2 * sy + 1, 1), :] = st[ACROSS_X[OUT[s]][1], face_x[s], pl.ds(ROW + sy - 1, 1), :]
 
     def edge_shares(step):
         a, b, c, d, e = packed([yb_out[step, j] for j in range(5)], None)
@@ -428,8 +427,9 @@
             for s in (0, 1):
                 if x == face_x[s]:
                     if step == 0:
-                        parts = face_reads(step, s, r)
+                        parts = face_raw(s, r)
                         shares = tree_sum(parts), parts[1] - parts[2], parts[3] - parts[4]
+                        face_reads(s, r, parts)
                     else:
                         shares = [xo_in[s, m, rows, :] for m in range(3)]
                     sums[0] = sums[0] + shares[0]
@@ -452,13 +452,20 @@
             peak = jnp.maximum(peak, speed[0] + speed[1] + speed[2])
         return peak
 
-    def face_reads(step, s, r):
-        parts = []
-        for j, k in enumerate(ACROSS_X[IN[s]]):
-            part = shift_z(xr[step, s, j, pl.ds(ROW + r - CS[k][1], ROW), :], CS[k][2])
+    def face_raw(s, r):
+        return [
+            shift_z(xr[s, j, pl.ds(ROW + r - CS[k][1], ROW), :], CS[k][2]) for j, k in enumerate(ACROSS_X[IN[s]])
+        ]
+
+    def face_rest(s, r):
+        total, along, height = (xo_in[s, m, pl.ds(r, ROW), :] for m in range(3))
+        b, d = x2_in[s, pl.ds(r, ROW), :], x2_in[s, pl.ds(sy + r, ROW), :]
+        c, e = b - along, d - height
+        return [total - ((b + c) + (d + e)), b, c, d, e]
+
+    def face_reads(s, r, parts):
+        for k, part in zip(ACROSS_X[IN[s]], parts):
             rd[k, face_x[s], pl.ds(r, ROW), :] = part
-            parts.append(part)
-        return parts
 
     def edge_reads():
         for s in (0, 1):
@@ -471,7 +478,10 @@
             j = 1 if OUT[xs] > 0 else 2
             tu[0, pl.ds(c, 1), :] = yb_in[step, j, pl.ds(ys * sx + face_x[xs], 1), :]
             j = 1 if OUT[ys] > 0 else 2
-            tu[1, pl.ds(c, 1), :] = xr[step, xs, j, pl.ds(ROW + edge_y[ys], 1), :]
+            if step == 0:
+                tu[1, pl.ds(c, 1), :] = xr[xs, j, pl.ds(ROW + edge_y[ys], 1), :]
+            else:
+                tu[1, pl.ds(c, 1), :] = x2_in[xs, pl.ds(2 * sy + ys, 1), :]
         over, up = tu[0], tu[1]
         total = cm_in[step, 0] + over
         for m, value in enumerate((total, cm_in[step, 1] - corner_x * over, corner_y * total, cm_in[step, 2])):
@@ -629,29 +639,44 @@
     load_p.wait()
     own_sums(0, blocks)
     pack_y_raw(0)
-    if not by_word:
-        corner_sums(0)
+    corner_sums(0)
     pl.semaphore_wait(barrier, partners)
     if by_word:
-        for dx, dy in column:
-            greet(in_sem, gx, lax.rem(gy + dy, ngy))
-    send_x_raw(0)
-    send_x_sums(0)
+        for s in (0, 1):
+
+            @pl.when(has_y[s])
+            def _():
+                greet(in_sem, gx, y_of[s])
+
+        for _, dy in column:
+            other = lax.rem(gy + dy, ngy)
+
+            @pl.when((other > gy + 1) | (other < gy - 1))
+            def _():
+                greet(col_sem, gx, other)
+
+    sums_far, sums_near = send_x_sums(0)
+    raw_far, raw_near = send_x_raw()
+    sums_far()
     send_y(0, raw_fields, yr_recv)
     send_y(0, sum_fields, ym_recv)
+    neighbours = jnp.where(has_up, 1, 0) + jnp.where(has_down, 1, 0)
     if by_word:
-        corner_sums(0)
-        pl.semaphore_wait(in_sem, len(column))
+        pl.semaphore_wait(in_sem, neighbours)
     send_corner_raw(0)
     send_corner_sums(0)
+    sums_near()
+    raw_far()
+    if by_word:
+        pl.semaphore_wait(col_sem, len(column) - neighbours)
+    raw_near()
     face_shares(0)
     edge_shares(0)
+    send_heat()
     await_y_raw(0)
-    await_x_raw(0)
+    await_x_raw()
     await_sums(0)
     finish_peak = spread_all(0, velocity_pass(0, None))
-    send_heat_x(hx_recv.at[0], True)
-    send_heat_y()
     edge_reads()
     ghost_pass(0, None)
 
@@ -660,22 +685,22 @@
 
     collided(outer, None, store_st1)
     face_shares(1)
-    send_x_shares()
+    shares_far, shares_near = send_x_shares()
+    shares_far()
     collided(inner, None, store_st1)
+    shares_near()
     send_corner_raw(1)
     pack_y_raw(1)
     send_y(1, raw_fields, yr_recv)
-    send_x_raw(1)
     own_sums(1, outer)
-    send_x_sums(1)
+    for part in (*send_x_sums(1), *send_x_rest()):
+        part()
     own_sums(1, inner)
     send_y(1, sum_fields, ym_recv)
     corner_sums(1)
     send_corner_sums(1)
-    send_heat_x(hx_recv.at[1], False)
-    send_heat_corner()
     edge_shares(1)
-    await_near_heat()
+    await_heat()
     near_heat()
     fs = finish_peak()
     await_y_raw(1)
@@ -684,12 +709,11 @@
     for x, r in blocks:
         for c in range(3):
             out_v[c, x, pl.ds(r, ROW), :] = vel[c, x + 1, pl.ds(ROW + r, ROW), :]
-    await_far_heat()
     far_heat()
-    await_x_raw(1)
+    await_x_rest()
     for s in (0, 1):
         for r in range(0, sy, ROW):
-            face_reads(1, s, r)
+            face_reads(s, r, face_rest(s, r))
     edge_reads()
     await_sums(1)
     ghost_pass(1, fs)
@@ -761,7 +785,7 @@
             floats(sx + 4, tall, nz),
             floats(4, sx + 2, sy, nz),
             floats(4, 2 * sx, nz),
-            floats(STEPS, 2, 5, tall, nz),
+            floats(2, 5, tall, nz),
             floats(STEPS, 2, 4, sy, nz),
             floats(STEPS, 2, 4, sy, nz),
             floats(STEPS, 9, 2 * sx, nz),
@@ -771,7 +795,9 @@
             floats(STEPS, ROW, nz),
             floats(STEPS, 6, ROW, nz),
             floats(2, 3, sy, nz),
+            floats(2, 2 * sy + ROW, nz),
             floats(2, 3, sy, nz),
+            floats(2, 2 * sy + ROW, nz),
             floats(4, 2 * sx, nz),
             floats(5, 2 * sx, nz),
             floats(4, 2 * sx, nz),
@@ -785,6 +811,7 @@
             *[floats(STEPS, -(-len(group) // ROW) * ROW, nz) for group in groups],
             dma((4,)),
             pltpu.SemaphoreType.REGULAR,
+            pltpu.SemaphoreType.REGULAR,
             dma,
             dma((2,)),
             dma((STEPS,)),
@@ -792,8 +819,7 @@
             dma,
             dma((STEPS, 2)),
             dma((STEPS, 2)),
-            dma((2,)),
-            dma((2,)),
+            dma,
             dma((2,)),
             dma((phases,)),
             dma((STEPS, phases)),

time: 22.2 us -> 21.3 us (0.959)
  Pallas kernels: 21.4 us -> 20.5 us
    pallas_call x1, Pallas kernels: 20.5 us -> 19.6 us  [local(): pl.pallas_call(functools.partial(kernel, ngx, ngy), out_shape=shapes, in_...]
where the time goes in v3:
time: 21.3 us; the launch traced here: 21.2 us
  Pallas kernels  20.5 us (96%)
  between operations  0.64 us (3%)
    pallas_call x1, Pallas kernels, local(): pl.pallas_call(functools.partial(kernel, ngx, ngy), out_shape=shapes, in_...  19.6 us
    pallas_call x1, Pallas kernels, local(): pl.pallas_call(write_out, out_shape=shapes, in_specs=[vmem] * 2, out_spec...  0.87 us

profile of v3, /device:TPU:0, one launch (start us, length us, event | category | flops | bytes accessed | tf_op | source)
XLA Modules:
  0.0 21.2 jit_solution(4789832708773109919)
XLA Ops:
  0.6 19.6 %lattice_steps.1 = (f32[19,4,16,128]{3,2,1,0:T(8,128)S(1)}, f32[3,4,16,128]{3,2,1,0:T(8,128)S(1)}) custom-call(f32[19,4,16,128]{3,2,1,0:T(8,128)} %pops.1, s32[4,16,128]{2,1,0:T(8,128)} %heat_level.1, s32[4,16,128]{2,1,0:T(8,128)} %obstacle.1, f32[8]{0:T(128)} %table.1), custom_call_target="tpu_custom_call" | custom-call | tf_op jit(solution)/shard_map/lattice_steps/pallas_call | solution.py:767
  20.3 0.9 %write_out.1 = (f32[19,4,16,128]{3,2,1,0:T(8,128)}, f32[3,4,16,128]{3,2,1,0:T(8,128)}) custom-call(f32[19,4,16,128]{3,2,1,0:T(8,128)S(1)} %get-tuple-element.4.pops, f32[3,4,16,128]{3,2,1,0:T(8,128)S(1)} %get-tuple-element.5.vel), custom_call_target="tpu_custom_call" | custom-call | tf_op jit(solution)/shard_map/write_out/pallas_call | solution.py:832

commit v4 on v3

--- a/solution.py
+++ b/solution.py
@@ -72,7 +72,7 @@
     ox, ox2, xo_in, x2_in, oy, dr, dm, tu, ex, ey, gfx, gfy, flat, pm_src, *rest,
 ):
     (*pm_bufs, load_sem, in_sem, col_sem, x_send, y_send, xr_recv, xm_recv, xo_recv, yr_recv, ym_recv,
-     hx_recv, hy_recv, p_send, p_recv) = rest
+     cm_recv, hx_recv, hy_recv, p_send, p_recv) = rest
     _, sx, sy, nz = pops.shape
     levels = table.shape[0]
     gx = lax.axis_index("gx")
@@ -169,36 +169,36 @@
 
     at_end = (gx == 0, gx == ngx - 1)
 
-    def along_x(pairs_of, recv_sem):
+    def along_x(pairs_of, sem_of):
         def far():
             for s in (0, 1):
-                send(at_end[s], pairs_of(s), x_send, recv_sem, x_of[s], gy)
+                send(at_end[s], pairs_of(s), x_send, sem_of(s), x_of[s], gy)
 
         def near():
             for s in (0, 1):
-                send(jnp.logical_not(at_end[s]), pairs_of(s), x_send, recv_sem, x_of[s], gy)
+                send(jnp.logical_not(at_end[s]), pairs_of(s), x_send, sem_of(s), x_of[s], gy)
 
         return far, near
 
     def send_x_raw():
         return along_x(
             lambda s: [(st0.at[k, face_x[s], own_y, :], xr.at[1 - s, j, own_y, :]) for j, k in enumerate(ACROSS_X[OUT[s]])],
-            xr_recv.at[0],
+            lambda s: xr_recv.at[0],
         )
 
     def send_x_sums(step):
-        return along_x(lambda s: [(xm_out.at[step, s], xm_in.at[step, 1 - s])], xm_recv.at[step])
+        return along_x(lambda s: [(xm_out.at[step, s], xm_in.at[step, 1 - s])], lambda s: xm_recv.at[step, 1 - s])
 
     rest_rows = pl.ds(0, 2 * sy + 2)
 
-    def send_x_shares():
-        return along_x(lambda s: [(ox.at[s], xo_in.at[1 - s])], xo_recv)
+    def send_x_shares(s):
+        send(None, [(ox.at[s], xo_in.at[1 - s])], x_send, xo_recv, x_of[s], gy)
 
     def send_x_rest():
-        return along_x(lambda s: [(ox2.at[s, rest_rows, :], x2_in.at[1 - s, rest_rows, :])], xr_recv.at[1])
+        return along_x(lambda s: [(ox2.at[s, rest_rows, :], x2_in.at[1 - s, rest_rows, :])], lambda s: xr_recv.at[1])
 
     def send_heat():
-        for part in along_x(lambda s: [(hb.at[pl.ds((2, sx)[s], 2), own_y, :], hb.at[pl.ds((sx + 2, 0)[s], 2), own_y, :])], hx_recv):
+        for part in along_x(lambda s: [(hb.at[pl.ds((2, sx)[s], 2), own_y, :], hb.at[pl.ds((sx + 2, 0)[s], 2), own_y, :])], lambda s: hx_recv):
             part()
         for s in (0, 1):
             src = hb.at[pl.ds(2, sx), pl.ds((ROW, ROW + sy - 2)[s], 2), :]
@@ -209,7 +209,7 @@
                 hb.at[2 + face_x[xs], pl.ds(ROW + edge_y[ys], 1), :],
                 hb.at[(sx + 2, 1)[xs], pl.ds((ROW + sy, ROW - 1)[ys], 1), :],
             ),
-            lambda s: hy_recv.at[s],
+            lambda c: hy_recv.at[c % 2],
         )
 
     def send_y(step, fields, recv_sem):
@@ -220,7 +220,7 @@
 
     def to_corners(pair_of, sem_of):
         for c, (xs, ys) in enumerate(corners):
-            send(has_y[ys], [pair_of(c, xs, ys)], y_send.at[ys], sem_of(1 - ys), x_of[xs], y_of[ys])
+            send(has_y[ys], [pair_of(c, xs, ys)], y_send.at[ys], sem_of(3 - c), x_of[xs], y_of[ys])
 
     def send_corner_raw(step):
         st = states[step]
@@ -229,12 +229,12 @@
             k = NUMBER[(OUT[xs], OUT[ys], 0)]
             return st.at[k, face_x[xs], pl.ds(ROW + edge_y[ys], 1), :], cr_in.at[step, pl.ds(3 - c, 1), :]
 
-        to_corners(pair, lambda s: yr_recv.at[step, s])
+        to_corners(pair, lambda c: yr_recv.at[step, c % 2])
 
     def send_corner_sums(step):
         to_corners(
             lambda c, xs, ys: (cm_out.at[step, :, pl.ds(c, 1), :], cm_in.at[step, :, pl.ds(3 - c, 1), :]),
-            lambda s: ym_recv.at[step, s],
+            lambda c: cm_recv.at[step, c],
         )
 
     def await_y_raw(step):
@@ -247,10 +247,14 @@
     def await_x_rest():
         await_bytes(None, x2_in.at[:, rest_rows, :], xr_recv.at[1])
 
-    def await_sums(step):
-        for s in (0, 1):
-            await_bytes(has_y[s], flat.at[pl.ds(0, 4 * sx + 12), :], ym_recv.at[step, s])
-        await_bytes(None, xm_in.at[step], xm_recv.at[step])
+    def await_y_sums(step):
+        for s in (0, 1):
+            await_bytes(has_y[s], yb_in.at[step, sum_fields, pl.ds(s * sx, sx), :], ym_recv.at[step, s])
+
+    def await_x_sums(step, s):
+        for ys in (0, 1):
+            await_bytes(has_y[ys], cm_in.at[step, :, pl.ds(2 * s + ys, 1), :], cm_recv.at[step, 2 * s + ys])
+        await_bytes(None, xm_in.at[step, s], xm_recv.at[step, s])
 
     def await_heat():
         for s in (0, 1):
@@ -272,7 +276,7 @@
         count = len(group)
         buf = pm_bufs[phase]
         pm_src[step, phase] = value
-        for d, (dx, dy) in enumerate(group, 1):
+        for d, (dx, dy) in sorted(enumerate(group, 1), key=lambda item: item[1][0] in (0, ngx // 2)):
             place = {"gx": lax.rem(gx + dx, ngx), "gy": lax.rem(gy + dy, ngy)}
             pltpu.make_async_remote_copy(
                 src_ref=pm_src.at[step, phase],
@@ -387,9 +391,9 @@
                 minus = jnp.where(pack_row == ys * sx + sx - 1, fill(2 + ys), minus)
         return [fields[0], plus, minus, shift_z(fields[3], 1), shift_z(fields[4], -1)]
 
-    def face_shares(step):
+    def face_shares(step, sides):
         st = states[step]
-        for s in (0, 1):
+        for s in sides:
             for r in range(0, sy, ROW):
                 ks = ACROSS_X[OUT[s]]
                 a, b, c, d, e = (st[k, face_x[s], pl.ds(ROW + r - CS[k][1], ROW), :] for k in ks)
@@ -473,44 +477,49 @@
                 for x in range(sx):
                     rd[k, x, pl.ds(edge_y[s], 1), :] = dr[j, pl.ds(s * sx + x, 1), :]
 
-    def ghost_pass(step, fs):
-        for c, (xs, ys) in enumerate(corners):
-            j = 1 if OUT[xs] > 0 else 2
-            tu[0, pl.ds(c, 1), :] = yb_in[step, j, pl.ds(ys * sx + face_x[xs], 1), :]
+    def ghost_x(step, fs, s):
+        own = pl.ds(2 * s, 2)
+        for ys in (0, 1):
+            c = 2 * s + ys
+            j = 1 if OUT[s] > 0 else 2
+            tu[0, pl.ds(c, 1), :] = yb_in[step, j, pl.ds(ys * sx + face_x[s], 1), :]
             j = 1 if OUT[ys] > 0 else 2
             if step == 0:
-                tu[1, pl.ds(c, 1), :] = xr[xs, j, pl.ds(ROW + edge_y[ys], 1), :]
+                tu[1, pl.ds(c, 1), :] = xr[s, j, pl.ds(ROW + edge_y[ys], 1), :]
             else:
-                tu[1, pl.ds(c, 1), :] = x2_in[xs, pl.ds(2 * sy + ys, 1), :]
-        over, up = tu[0], tu[1]
-        total = cm_in[step, 0] + over
-        for m, value in enumerate((total, cm_in[step, 1] - corner_x * over, corner_y * total, cm_in[step, 2])):
-            ex[m] = value
-        total = cm_in[step, 3] + up
-        for m, value in enumerate((total, corner_x * total, cm_in[step, 4] - corner_y * up, cm_in[step, 5])):
-            for c, (xs, ys) in enumerate(corners):
-                ey[m, pl.ds(ys * sx + face_x[xs], 1), :] = value[c : c + 1, :]
-        for s in (0, 1):
-            for r in range(0, sy, ROW):
-                rows = pl.ds(r, ROW)
-                share = ox[s, 0, rows, :]
-                sums = [xm_in[step, s, m, rows, :] for m in range(4)]
-                if step == 0:
-                    gfx[s, rows, :] = sums[0]
-                fluid = gfx[s, rows, :] > 0.0
-                sums[0] = sums[0] + share
-                sums[1] = sums[1] - share if s == 0 else sums[1] + share
-                sums[2] = sums[2] + ox[s, 1, rows, :]
-                sums[3] = sums[3] + ox[s, 2, rows, :]
-                for ys in edges_of(r):
-                    for m in range(4):
-                        sums[m] = sums[m] + jnp.where(edge_row[ys], ex[m, pl.ds(s * 2 + ys, 1), :], 0.0)
-                at = (0, sx + 1)[s]
-                if fs is not None:
-                    sums = [sums[m] + fs * hm[m, at, rows, :] for m in range(4)]
-                inv = jnp.where(fluid, 1.0 / jnp.where(fluid, sums[0], 1.0), 0.0)
-                for c in range(3):
-                    vel[c, at, pl.ds(ROW + r, ROW), :] = sums[1 + c] * inv
+                tu[1, pl.ds(c, 1), :] = x2_in[s, pl.ds(2 * sy + ys, 1), :]
+        sums = [cm_in[step, m, own, :] for m in range(6)]
+        over, up = tu[0, own, :], tu[1, own, :]
+        sign = jnp.where(lax.broadcasted_iota(jnp.int32, (2, nz), 0) == 0, 1.0, -1.0)
+        total = sums[0] + over
+        for m, value in enumerate((total, sums[1] + OUT[s] * over, sign * total, sums[2])):
+            ex[m, own, :] = value
+        total = sums[3] + up
+        for m, value in enumerate((total, IN[s] * total, sums[4] - sign * up, sums[5])):
+            for ys in (0, 1):
+                ey[m, pl.ds(ys * sx + face_x[s], 1), :] = value[ys : ys + 1, :]
+        for r in range(0, sy, ROW):
+            rows = pl.ds(r, ROW)
+            share = ox[s, 0, rows, :]
+            sums = [xm_in[step, s, m, rows, :] for m in range(4)]
+            if step == 0:
+                gfx[s, rows, :] = sums[0]
+            fluid = gfx[s, rows, :] > 0.0
+            sums[0] = sums[0] + share
+            sums[1] = sums[1] - share if s == 0 else sums[1] + share
+            sums[2] = sums[2] + ox[s, 1, rows, :]
+            sums[3] = sums[3] + ox[s, 2, rows, :]
+            for ys in edges_of(r):
+                for m in range(4):
+                    sums[m] = sums[m] + jnp.where(edge_row[ys], ex[m, pl.ds(s * 2 + ys, 1), :], 0.0)
+            at = (0, sx + 1)[s]
+            if fs is not None:
+                sums = [sums[m] + fs * hm[m, at, rows, :] for m in range(4)]
+            inv = jnp.where(fluid, 1.0 / jnp.where(fluid, sums[0], 1.0), 0.0)
+            for c in range(3):
+                vel[c, at, pl.ds(ROW + r, ROW), :] = sums[1 + c] * inv
+
+    def ghost_y(step, fs):
         sums = [yb_in[step, 5 + m] for m in range(4)]
         if step == 0:
             gfy[...] = sums[0]
@@ -657,38 +666,49 @@
 
     sums_far, sums_near = send_x_sums(0)
     raw_far, raw_near = send_x_raw()
+    neighbours = jnp.where(has_up, 1, 0) + jnp.where(has_down, 1, 0)
+    raw_far()
     sums_far()
     send_y(0, raw_fields, yr_recv)
     send_y(0, sum_fields, ym_recv)
-    neighbours = jnp.where(has_up, 1, 0) + jnp.where(has_down, 1, 0)
     if by_word:
         pl.semaphore_wait(in_sem, neighbours)
     send_corner_raw(0)
     send_corner_sums(0)
-    sums_near()
-    raw_far()
     if by_word:
         pl.semaphore_wait(col_sem, len(column) - neighbours)
     raw_near()
-    face_shares(0)
+    sums_near()
+    face_shares(0, (0, 1))
     edge_shares(0)
     send_heat()
     await_y_raw(0)
     await_x_raw()
-    await_sums(0)
     finish_peak = spread_all(0, velocity_pass(0, None))
     edge_reads()
-    ghost_pass(0, None)
+    await_y_sums(0)
 
     def store_st1(k, x, r, value):
         st1[k, x, pl.ds(ROW + r, ROW), :] = value
 
-    collided(outer, None, store_st1)
-    face_shares(1)
-    shares_far, shares_near = send_x_shares()
-    shares_far()
+    def faces(sides):
+        for s in sides:
+            await_x_sums(0, s)
+            ghost_x(0, None, s)
+            ghost_y(0, None)
+            collided([(x, r) for x, r in blocks if x == face_x[s]], None, store_st1)
+            face_shares(1, (s,))
+            send_x_shares(s)
+
+    @pl.when(gx == ngx - 1)
+    def _():
+        faces((1, 0))
+
+    @pl.when(gx != ngx - 1)
+    def _():
+        faces((0, 1))
+
     collided(inner, None, store_st1)
-    shares_near()
     send_corner_raw(1)
     pack_y_raw(1)
     send_y(1, raw_fields, yr_recv)
@@ -715,8 +735,11 @@
         for r in range(0, sy, ROW):
             face_reads(s, r, face_rest(s, r))
     edge_reads()
-    await_sums(1)
-    ghost_pass(1, fs)
+    await_y_sums(1)
+    for s in (0, 1):
+        await_x_sums(1, s)
+        ghost_x(1, fs, s)
+    ghost_y(1, fs)
 
     def store_out(k, x, r, value):
         out_p[k, x, pl.ds(r, ROW), :] = value
@@ -815,10 +838,11 @@
             dma,
             dma((2,)),
             dma((STEPS,)),
-            dma((STEPS,)),
+            dma((STEPS, 2)),
             dma,
             dma((STEPS, 2)),
             dma((STEPS, 2)),
+            dma((STEPS, 4)),
             dma,
             dma((2,)),
             dma((phases,)),

time: 21.3 us -> 20.8 us (0.977)
  Pallas kernels: 20.5 us -> 20 us
    pallas_call x1, Pallas kernels: 19.6 us -> 19.1 us  [local(): pl.pallas_call(functools.partial(kernel, ngx, ngy), out_shape=shapes, in_...]
where the time goes in v4:
time: 20.8 us; the launch traced here: 20.6 us
  Pallas kernels  20 us (96%)
  between operations  0.64 us (3%)
    pallas_call x1, Pallas kernels, local(): pl.pallas_call(functools.partial(kernel, ngx, ngy), out_shape=shapes, in_...  19.1 us
    pallas_call x1, Pallas kernels, local(): pl.pallas_call(write_out, out_shape=shapes, in_specs=[vmem] * 2, out_spec...  0.87 us

profile of v4, /device:TPU:0, one launch (start us, length us, event | category | flops | bytes accessed | tf_op | source)
XLA Modules:
  0.0 20.6 jit_solution(5693897381634390362)
XLA Ops:
  0.6 19.1 %lattice_steps.1 = (f32[19,4,16,128]{3,2,1,0:T(8,128)S(1)}, f32[3,4,16,128]{3,2,1,0:T(8,128)S(1)}) custom-call(f32[19,4,16,128]{3,2,1,0:T(8,128)} %pops.1, s32[4,16,128]{2,1,0:T(8,128)} %heat_level.1, s32[4,16,128]{2,1,0:T(8,128)} %obstacle.1, f32[8]{0:T(128)} %table.1), custom_call_target="tpu_custom_call" | custom-call | tf_op jit(solution)/shard_map/lattice_steps/pallas_call | solution.py:790
  19.7 0.9 %write_out.1 = (f32[19,4,16,128]{3,2,1,0:T(8,128)}, f32[3,4,16,128]{3,2,1,0:T(8,128)}) custom-call(f32[19,4,16,128]{3,2,1,0:T(8,128)S(1)} %get-tuple-element.4.pops, f32[3,4,16,128]{3,2,1,0:T(8,128)S(1)} %get-tuple-element.5.vel), custom_call_target="tpu_custom_call" | custom-call | tf_op jit(solution)/shard_map/write_out/pallas_call | solution.py:856

commit v5 on v4

--- a/solution.py
+++ b/solution.py
@@ -68,7 +68,7 @@
     out_p, out_v,
     st0, st1, rd, ms, rho_s, vel, hl, ob, tb, solid_s,
     hb, hzp, hzm, hm, hmy,
-    xr, xm_out, xm_in, yb_out, yb_in, cg, cm_out, cr_in, cm_in,
+    xr, xp, xm_out, xm_in, yb_out, yb_in, cg, cm_out, cr_in, cm_in,
     ox, ox2, xo_in, x2_in, oy, dr, dm, tu, ex, ey, gfx, gfy, flat, pm_src, *rest,
 ):
     (*pm_bufs, load_sem, in_sem, col_sem, x_send, y_send, xr_recv, xm_recv, xo_recv, yr_recv, ym_recv,
@@ -182,7 +182,7 @@
 
     def send_x_raw():
         return along_x(
-            lambda s: [(st0.at[k, face_x[s], own_y, :], xr.at[1 - s, j, own_y, :]) for j, k in enumerate(ACROSS_X[OUT[s]])],
+            lambda s: [(xp.at[s], xr.at[1 - s, :, own_y, :])],
             lambda s: xr_recv.at[0],
         )
 
@@ -197,9 +197,13 @@
     def send_x_rest():
         return along_x(lambda s: [(ox2.at[s, rest_rows, :], x2_in.at[1 - s, rest_rows, :])], lambda s: xr_recv.at[1])
 
+    def send_heat_x(layer):
+        src, dst = ((2, sx + 1), (sx + 2, 1)) if layer == 0 else ((3, sx), (sx + 3, 0))
+        for s in (0, 1):
+            send(None, [(hb.at[src[s], own_y, :], hb.at[dst[s], own_y, :])], x_send, hx_recv.at[layer], x_of[s], gy)
+
     def send_heat():
-        for part in along_x(lambda s: [(hb.at[pl.ds((2, sx)[s], 2), own_y, :], hb.at[pl.ds((sx + 2, 0)[s], 2), own_y, :])], lambda s: hx_recv):
-            part()
+        send_heat_x(0)
         for s in (0, 1):
             src = hb.at[pl.ds(2, sx), pl.ds((ROW, ROW + sy - 2)[s], 2), :]
             dst = hb.at[pl.ds(2, sx), pl.ds((ROW + sy, ROW - 2)[s], 2), :]
@@ -259,10 +263,10 @@
     def await_heat():
         for s in (0, 1):
             await_bytes(has_y[s], flat.at[pl.ds(0, 2 * sx + 2), :], hy_recv.at[s])
-        await_bytes(None, hb.at[pl.ds(0, 4), own_y, :], hx_recv)
+        await_bytes(None, hb.at[pl.ds(0, 2), own_y, :], hx_recv.at[0])
 
     def await_sends():
-        for view in (xr.at[:, :, own_y, :], xm_out, ox, ox2.at[:, rest_rows, :], hb.at[pl.ds(0, 4), own_y, :]):
+        for view in (xp, xm_out, ox, ox2.at[:, rest_rows, :], hb.at[pl.ds(0, 4), own_y, :]):
             await_bytes(None, view, x_send)
         for s in (0, 1):
             for view in (yb_out.at[:, :, pl.ds(0, sx), :], flat.at[pl.ds(0, 2 * sx + STEPS * 14 + 2), :]):
@@ -357,6 +361,11 @@
                     for m in range(4):
                         yb_out[step, 5 + m, pl.ds(s * sx + x, 1), :] = sums[m][at : at + 1, :]
 
+    def pack_x_raw():
+        for s in (0, 1):
+            for j, k in enumerate(ACROSS_X[OUT[s]]):
+                xp[s, j] = st0[k, face_x[s], own_y, :]
+
     def pack_y_raw(step):
         st = states[step]
         for s in (0, 1):
@@ -416,7 +425,7 @@
         oy[2] = -pack_sign * total
         oy[3] = d - e
 
-    def velocity_pass(step, fs):
+    def edge_moments(step):
         fields = packed([yb_in[step, j] for j in range(5)], lambda c: cr_in[step, pl.ds(c, 1), :])
         for j in range(5):
             dr[j] = fields[j]
@@ -424,8 +433,9 @@
         total = ((a + b) + (c + d)) + e
         for m, value in enumerate((total, b - c, pack_sign * total, d - e)):
             dm[m] = value
-        peak = jnp.zeros((ROW, nz), jnp.float32)
-        for x, r in blocks:
+
+    def velocity_pass(step, fs, tiles, peak):
+        for x, r in tiles:
             rows = pl.ds(r, ROW)
             sums = [ms[m, x, rows, :] for m in range(4)]
             for s in (0, 1):
@@ -645,10 +655,14 @@
         solid_s[x, rows, :] = jnp.where(solid, 1, 0)
         hb[x + 2, pl.ds(ROW + r, ROW), :] = jnp.where(solid, 0.0, heat)
 
+    neighbours = jnp.where(has_up, 1, 0) + jnp.where(has_down, 1, 0)
+    sums_far, sums_near = send_x_sums(0)
+    raw_far, raw_near = send_x_raw()
+    neighbours = jnp.where(has_up, 1, 0) + jnp.where(has_down, 1, 0)
+    sums_far, sums_near = send_x_sums(0)
+    raw_far, raw_near = send_x_raw()
     load_p.wait()
-    own_sums(0, blocks)
-    pack_y_raw(0)
-    corner_sums(0)
+    pack_x_raw()
     pl.semaphore_wait(barrier, partners)
     if by_word:
         for s in (0, 1):
@@ -657,6 +671,10 @@
             def _():
                 greet(in_sem, gx, y_of[s])
 
+    raw_far()
+    own_sums(0, outer)
+    sums_far()
+    if by_word:
         for _, dy in column:
             other = lax.rem(gy + dy, ngy)
 
@@ -664,12 +682,10 @@
             def _():
                 greet(col_sem, gx, other)
 
-    sums_far, sums_near = send_x_sums(0)
-    raw_far, raw_near = send_x_raw()
-    neighbours = jnp.where(has_up, 1, 0) + jnp.where(has_down, 1, 0)
-    raw_far()
-    sums_far()
+    pack_y_raw(0)
     send_y(0, raw_fields, yr_recv)
+    corner_sums(0)
+    own_sums(0, inner)
     send_y(0, sum_fields, ym_recv)
     if by_word:
         pl.semaphore_wait(in_sem, neighbours)
@@ -682,31 +698,35 @@
     face_shares(0, (0, 1))
     edge_shares(0)
     send_heat()
+    no_peak = jnp.zeros((ROW, nz), jnp.float32)
     await_y_raw(0)
+    edge_moments(0)
+    peak = velocity_pass(0, None, inner, no_peak)
     await_x_raw()
-    finish_peak = spread_all(0, velocity_pass(0, None))
+    finish_peak = spread_all(0, velocity_pass(0, None, outer, peak))
     edge_reads()
     await_y_sums(0)
 
     def store_st1(k, x, r, value):
         st1[k, x, pl.ds(ROW + r, ROW), :] = value
 
-    def faces(sides):
-        for s in sides:
-            await_x_sums(0, s)
-            ghost_x(0, None, s)
-            ghost_y(0, None)
-            collided([(x, r) for x, r in blocks if x == face_x[s]], None, store_st1)
-            face_shares(1, (s,))
-            send_x_shares(s)
+    def face(s):
+        await_x_sums(0, s)
+        ghost_x(0, None, s)
+        ghost_y(0, None)
+        collided([(x, r) for x, r in blocks if x == face_x[s]], None, store_st1)
+        face_shares(1, (s,))
+        send_x_shares(s)
 
     @pl.when(gx == ngx - 1)
     def _():
-        faces((1, 0))
+        face(1)
+        face(0)
 
     @pl.when(gx != ngx - 1)
     def _():
-        faces((0, 1))
+        face(0)
+        face(1)
 
     collided(inner, None, store_st1)
     send_corner_raw(1)
@@ -719,16 +739,20 @@
     send_y(1, sum_fields, ym_recv)
     corner_sums(1)
     send_corner_sums(1)
+    send_heat_x(1)
     edge_shares(1)
     await_heat()
     near_heat()
     fs = finish_peak()
     await_y_raw(1)
+    edge_moments(1)
+    peak = velocity_pass(1, fs, inner, no_peak)
     await_bytes(None, xo_in, xo_recv)
-    finish_peak = spread_all(1, velocity_pass(1, fs))
+    finish_peak = spread_all(1, velocity_pass(1, fs, outer, peak))
     for x, r in blocks:
         for c in range(3):
             out_v[c, x, pl.ds(r, ROW), :] = vel[c, x + 1, pl.ds(ROW + r, ROW), :]
+    await_bytes(None, hb.at[pl.ds(0, 2), own_y, :], hx_recv.at[1])
     far_heat()
     await_x_rest()
     for s in (0, 1):
@@ -809,6 +833,7 @@
             floats(4, sx + 2, sy, nz),
             floats(4, 2 * sx, nz),
             floats(2, 5, tall, nz),
+            floats(2, 5, sy, nz),
             floats(STEPS, 2, 4, sy, nz),
             floats(STEPS, 2, 4, sy, nz),
             floats(STEPS, 9, 2 * sx, nz),
@@ -843,7 +868,7 @@
             dma((STEPS, 2)),
             dma((STEPS, 2)),
             dma((STEPS, 4)),
-            dma,
+            dma((2,)),
             dma((2,)),
             dma((phases,)),
             dma((STEPS, phases)),

time: 20.8 us -> 20.6 us (level)
  no operation moved by 1% of the time
where the time goes in v5:
time: 20.6 us; the launch traced here: 20.4 us
  Pallas kernels  19.8 us (96%)
  between operations  0.64 us (3%)
    pallas_call x1, Pallas kernels, local(): pl.pallas_call(functools.partial(kernel, ngx, ngy), out_shape=shapes, in_...  18.9 us
    pallas_call x1, Pallas kernels, local(): pl.pallas_call(write_out, out_shape=shapes, in_specs=[vmem] * 2, out_spec...  0.87 us

profile of v5, /device:TPU:0, one launch (start us, length us, event | category | flops | bytes accessed | tf_op | source)
XLA Modules:
  0.0 20.4 jit_solution(7286413925153139413)
XLA Ops:
  0.6 18.9 %lattice_steps.1 = (f32[19,4,16,128]{3,2,1,0:T(8,128)S(1)}, f32[3,4,16,128]{3,2,1,0:T(8,128)S(1)}) custom-call(f32[19,4,16,128]{3,2,1,0:T(8,128)} %pops.1, s32[4,16,128]{2,1,0:T(8,128)} %heat_level.1, s32[4,16,128]{2,1,0:T(8,128)} %obstacle.1, f32[8]{0:T(128)} %table.1), custom_call_target="tpu_custom_call" | custom-call | tf_op jit(solution)/shard_map/lattice_steps/pallas_call | solution.py:814
  19.5 0.9 %write_out.1 = (f32[19,4,16,128]{3,2,1,0:T(8,128)}, f32[3,4,16,128]{3,2,1,0:T(8,128)}) custom-call(f32[19,4,16,128]{3,2,1,0:T(8,128)S(1)} %get-tuple-element.4.pops, f32[3,4,16,128]{3,2,1,0:T(8,128)S(1)} %get-tuple-element.5.vel), custom_call_target="tpu_custom_call" | custom-call | tf_op jit(solution)/shard_map/write_out/pallas_call | solution.py:881

commit v6 on v5

--- a/solution.py
+++ b/solution.py
@@ -271,6 +271,8 @@
         for s in (0, 1):
             for view in (yb_out.at[:, :, pl.ds(0, sx), :], flat.at[pl.ds(0, 2 * sx + STEPS * 14 + 2), :]):
                 await_bytes(has_y[s], view, y_send.at[s])
+
+    def await_peak_sends():
         for phase, group in enumerate(groups):
             for step in range(STEPS):
                 await_bytes(None, pm_bufs[phase].at[step, pl.ds(0, len(group)), :], p_send.at[phase])
@@ -771,6 +773,7 @@
     collided(blocks, fs, store_out)
     await_sends()
     fs = finish_peak()
+    await_peak_sends()
     lift = {(x, r): fs * hb[x + 2, pl.ds(ROW + r, ROW), :] for x, r in blocks}
     for k in LIFTED:
         for x, r in blocks:

time: 20.6 us -> 20.6 us (level)
  no operation moved by 1% of the time
where the time goes in v6:
time: 20.6 us; the launch traced here: 20.4 us
  Pallas kernels  19.8 us (96%)
  between operations  0.64 us (3%)
    pallas_call x1, Pallas kernels, local(): pl.pallas_call(functools.partial(kernel, ngx, ngy), out_shape=shapes, in_...  18.9 us
    pallas_call x1, Pallas kernels, local(): pl.pallas_call(write_out, out_shape=shapes, in_specs=[vmem] * 2, out_spec...  0.87 us

profile of v6, /device:TPU:0, one launch (start us, length us, event | category | flops | bytes accessed | tf_op | source)
XLA Modules:
  0.0 20.4 jit_solution(11628582051202612647)
XLA Ops:
  0.6 18.9 %lattice_steps.1 = (f32[19,4,16,128]{3,2,1,0:T(8,128)S(1)}, f32[3,4,16,128]{3,2,1,0:T(8,128)S(1)}) custom-call(f32[19,4,16,128]{3,2,1,0:T(8,128)} %pops.1, s32[4,16,128]{2,1,0:T(8,128)} %heat_level.1, s32[4,16,128]{2,1,0:T(8,128)} %obstacle.1, f32[8]{0:T(128)} %table.1), custom_call_target="tpu_custom_call" | custom-call | tf_op jit(solution)/shard_map/lattice_steps/pallas_call | solution.py:817
  19.5 0.9 %write_out.1 = (f32[19,4,16,128]{3,2,1,0:T(8,128)}, f32[3,4,16,128]{3,2,1,0:T(8,128)}) custom-call(f32[19,4,16,128]{3,2,1,0:T(8,128)S(1)} %get-tuple-element.4.pops, f32[3,4,16,128]{3,2,1,0:T(8,128)S(1)} %get-tuple-element.5.vel), custom_call_target="tpu_custom_call" | custom-call | tf_op jit(solution)/shard_map/write_out/pallas_call | solution.py:884

commit v7 on v6

--- a/solution.py
+++ b/solution.py
@@ -222,18 +222,19 @@
             dst = yb_in.at[step, fields, pl.ds((1 - s) * sx, sx), :]
             send(has_y[s], [(src, dst)], y_send.at[s], recv_sem.at[step, 1 - s], gx, y_of[s])
 
-    def to_corners(pair_of, sem_of):
+    def to_corners(pair_of, sem_of, sides=(0, 1)):
         for c, (xs, ys) in enumerate(corners):
-            send(has_y[ys], [pair_of(c, xs, ys)], y_send.at[ys], sem_of(3 - c), x_of[xs], y_of[ys])
-
-    def send_corner_raw(step):
+            if xs in sides:
+                send(has_y[ys], [pair_of(c, xs, ys)], y_send.at[ys], sem_of(3 - c), x_of[xs], y_of[ys])
+
+    def send_corner_raw(step, sides):
         st = states[step]
 
         def pair(c, xs, ys):
             k = NUMBER[(OUT[xs], OUT[ys], 0)]
             return st.at[k, face_x[xs], pl.ds(ROW + edge_y[ys], 1), :], cr_in.at[step, pl.ds(3 - c, 1), :]
 
-        to_corners(pair, lambda c: yr_recv.at[step, c % 2])
+        to_corners(pair, lambda c: yr_recv.at[step, c % 2], sides)
 
     def send_corner_sums(step):
         to_corners(
@@ -691,7 +692,7 @@
     send_y(0, sum_fields, ym_recv)
     if by_word:
         pl.semaphore_wait(in_sem, neighbours)
-    send_corner_raw(0)
+    send_corner_raw(0, (0, 1))
     send_corner_sums(0)
     if by_word:
         pl.semaphore_wait(col_sem, len(column) - neighbours)
@@ -717,6 +718,7 @@
         ghost_x(0, None, s)
         ghost_y(0, None)
         collided([(x, r) for x, r in blocks if x == face_x[s]], None, store_st1)
+        send_corner_raw(1, (s,))
         face_shares(1, (s,))
         send_x_shares(s)
 
@@ -731,7 +733,6 @@
         face(1)
 
     collided(inner, None, store_st1)
-    send_corner_raw(1)
     pack_y_raw(1)
     send_y(1, raw_fields, yr_recv)
     own_sums(1, outer)

time: 20.6 us -> 20.6 us (level)
  no operation moved by 1% of the time
where the time goes in v7:
time: 20.6 us; the launch traced here: 20.4 us
  Pallas kernels  19.8 us (96%)
  between operations  0.64 us (3%)
    pallas_call x1, Pallas kernels, local(): pl.pallas_call(functools.partial(kernel, ngx, ngy), out_shape=shapes, in_...  18.9 us
    pallas_call x1, Pallas kernels, local(): pl.pallas_call(write_out, out_shape=shapes, in_specs=[vmem] * 2, out_spec...  0.87 us

profile of v7, /device:TPU:0, one launch (start us, length us, event | category | flops | bytes accessed | tf_op | source)
XLA Modules:
  0.0 20.4 jit_solution(8929931123038116805)
XLA Ops:
  0.6 18.9 %lattice_steps.1 = (f32[19,4,16,128]{3,2,1,0:T(8,128)S(1)}, f32[3,4,16,128]{3,2,1,0:T(8,128)S(1)}) custom-call(f32[19,4,16,128]{3,2,1,0:T(8,128)} %pops.1, s32[4,16,128]{2,1,0:T(8,128)} %heat_level.1, s32[4,16,128]{2,1,0:T(8,128)} %obstacle.1, f32[8]{0:T(128)} %table.1), custom_call_target="tpu_custom_call" | custom-call | tf_op jit(solution)/shard_map/lattice_steps/pallas_call | solution.py:818
  19.5 0.9 %write_out.1 = (f32[19,4,16,128]{3,2,1,0:T(8,128)}, f32[3,4,16,128]{3,2,1,0:T(8,128)}) custom-call(f32[19,4,16,128]{3,2,1,0:T(8,128)S(1)} %get-tuple-element.4.pops, f32[3,4,16,128]{3,2,1,0:T(8,128)S(1)} %get-tuple-element.5.vel), custom_call_target="tpu_custom_call" | custom-call | tf_op jit(solution)/shard_map/write_out/pallas_call | solution.py:885

commit v8 on v7

--- a/solution.py
+++ b/solution.py
@@ -736,7 +736,7 @@
     pack_y_raw(1)
     send_y(1, raw_fields, yr_recv)
     own_sums(1, outer)
-    for part in (*send_x_sums(1), *send_x_rest()):
+    for part in (*send_x_rest(), *send_x_sums(1)):
         part()
     own_sums(1, inner)
     send_y(1, sum_fields, ym_recv)

time: 20.6 us -> 20.6 us (level)
  no operation moved by 1% of the time
where the time goes in v8:
time: 20.6 us; the launch traced here: 20.4 us
  Pallas kernels  19.8 us (96%)
  between operations  0.64 us (3%)
    pallas_call x1, Pallas kernels, local(): pl.pallas_call(functools.partial(kernel, ngx, ngy), out_shape=shapes, in_...  18.9 us
    pallas_call x1, Pallas kernels, local(): pl.pallas_call(write_out, out_shape=shapes, in_specs=[vmem] * 2, out_spec...  0.87 us

profile of v8, /device:TPU:0, one launch (start us, length us, event | category | flops | bytes accessed | tf_op | source)
XLA Modules:
  0.0 20.4 jit_solution(11800752551964219375)
XLA Ops:
  0.6 18.9 %lattice_steps.1 = (f32[19,4,16,128]{3,2,1,0:T(8,128)S(1)}, f32[3,4,16,128]{3,2,1,0:T(8,128)S(1)}) custom-call(f32[19,4,16,128]{3,2,1,0:T(8,128)} %pops.1, s32[4,16,128]{2,1,0:T(8,128)} %heat_level.1, s32[4,16,128]{2,1,0:T(8,128)} %obstacle.1, f32[8]{0:T(128)} %table.1), custom_call_target="tpu_custom_call" | custom-call | tf_op jit(solution)/shard_map/lattice_steps/pallas_call | solution.py:818
  19.5 0.9 %write_out.1 = (f32[19,4,16,128]{3,2,1,0:T(8,128)}, f32[3,4,16,128]{3,2,1,0:T(8,128)}) custom-call(f32[19,4,16,128]{3,2,1,0:T(8,128)S(1)} %get-tuple-element.4.pops, f32[3,4,16,128]{3,2,1,0:T(8,128)S(1)} %get-tuple-element.5.vel), custom_call_target="tpu_custom_call" | custom-call | tf_op jit(solution)/shard_map/write_out/pallas_call | solution.py:885
